TPU v7x, 256 devices: a 4x2x16 block of a 4x16x16 slice. The times are simulated.
256 devices in a mesh: groups: 2 (over y), dp: 16 (over z), section: 4 (over x), tensor: 2 (over core).
Axes of the slice: x: 4, y: 2, z: 16, core: 2. Of those that a mesh axis runs over, the one named last changes fastest.
The devices are a block of a 4x16x16 slice.
Arguments:
- hidden: bfloat16 [512, 8, 5120], P(('groups', 'dp')), parts along dimension 0, may hold values from -6 to 6
- unembed: bfloat16 [512, 8, 5120], P(('groups', 'dp')), parts along dimension 0, may hold values from -0.02734375 to 0.02734375
- value_proj: bfloat16 [4, 5120, 512], P('section', 'dp', 'tensor'), may hold values from -0.078125 to 0.078125
- output_proj: bfloat16 [4, 512, 5120], P('section', 'tensor', 'dp'), may hold values from -0.125 to 0.125
- norm_gains: float32 [4, 5120], P('section'), may hold values from 0.1 to 1.9
- survive: int32 [32], P(('groups', 'dp')), parts along dimension 0, may hold values from 0 to 1, as said below
- lengths: int32 [512], P(('groups', 'dp')), parts along dimension 0, may hold values from 1 to 8
- assign: int32 [512], P(('groups', 'dp')), parts along dimension 0, may hold values from 0 to 16, as said below
- advantage: float32 [512], P(('groups', 'dp')), parts along dimension 0, may hold values from -4 to 4
- reference_logit: float32 [512, 8], P(('groups', 'dp')), parts along dimension 0, may hold values from -4 to 4
- recorded_gap: float32 [512, 8], P(('groups', 'dp')), parts along dimension 0, may hold values from -2 to 2
Outputs:
- grad_value: float32 [8, 5120, 512], P(('groups', 'section'), 'dp', 'tensor'), parts along dimension 0
- grad_output: float32 [8, 512, 5120], P(('groups', 'section'), 'tensor', 'dp'), parts along dimension 0
There are 2 independent parts, one for each index of `groups`. A program takes and returns all parts, laid end to end along the dimension named above; an argument that names none is the same for every part. Nothing has to cross between parts.
Inputs may be any that keep to these rules, and one draw needn't show every extreme that they name: `survive`: 1 where the group of 16 responses is kept, 0 where it is dropped; in every draw all groups of some dp index are kept. `assign`: the 16 slots of a dp index list the local positions (0 to 15) of the responses of its kept groups, each exactly once, then hold 16 in every other slot.
All inputs are finite; a program needn't handle non-finite values.
Results may differ from a plain program's by a relative error of at most 0.029.
Values may be sent and summed in bfloat16 or wider, within the bound.
A program may use at most 64 MiB of HBM per device.

v0:
```python
import math

import jax
import jax.numpy as jnp
from jax import lax
from jax.sharding import PartitionSpec as P

GROUP = 16
MB_RESP = 8


eps_norm = 1e-06
loss_scale = 4096.0
clip_high = math.log(1.28)
clip_low = math.log(0.8)


def turned_gather(arrays, axis, dims):
    turned = [jnp.moveaxis(a, dim, 0) for a, dim in zip(arrays, dims)]
    widths = [t[0].size for t in turned]
    both = jnp.concatenate([t.reshape(-1, w) for t, w in zip(turned, widths)], axis=1)
    result = lax.all_gather(both, axis, axis=0, tiled=True)
    tiles = jnp.split(result, [sum(widths[:k]) for k in range(1, len(widths))], axis=1)
    return tuple(
        (
            jnp.moveaxis(b.reshape(-1, *t.shape[1:]), 0, dim)
            for b, t, dim in zip(tiles, turned, dims)
        )
    )


def copy_for_each(array, axis):
    devices = lax.axis_size(axis)
    return lax.all_to_all(
        jnp.broadcast_to(array[None], (devices, *array.shape)), axis, 0, 0, tiled=True
    )


def taken_together(array, axis):
    return copy_for_each(array, axis).astype(jnp.float32).sum(axis=0)


def from_behind(block, axis, distance):
    devices = range(lax.axis_size(axis))
    route = [(i - distance, i) for i in devices if i - distance in devices]
    return lax.ppermute(block, axis, route)


def of_everyone(array, axis):
    everything = copy_for_each(array, axis)
    return jnp.sum(everything, axis=0)


def norm_forward(row_block, norm_gain):
    values = row_block.astype(jnp.float32)
    inverse = lax.rsqrt(jnp.mean(values * values, axis=-1, keepdims=True) + eps_norm)
    return (values, inverse, (values * inverse * norm_gain).astype(jnp.bfloat16))


def norm_backward(values, inverse, norm_gain, upstream):
    scaled = upstream * norm_gain
    inner_sum = jnp.sum(scaled * values, axis=-1, keepdims=True) / values.shape[-1]
    return inverse * scaled - values * (inverse * inverse * inverse) * inner_sum


def contract_last(left_rows, right_rows):
    return lax.dot_general(
        left_rows, right_rows, (((1,), (1,)), ((), ())), preferred_element_type=jnp.float32
    )


def contract_first(left_rows, right_rows):
    return lax.dot_general(
        left_rows, right_rows, (((0,), (0,)), ((), ())), preferred_element_type=jnp.float32
    )


def take_slot(slot_store, slot_index):
    return lax.dynamic_index_in_dim(slot_store, slot_index, 0, keepdims=False)


def put_slot(slot_store, new_value, slot_index, active):
    previous = take_slot(slot_store, slot_index)
    return lax.dynamic_update_index_in_dim(
        slot_store, jnp.where(active, new_value, previous), slot_index, 0
    )


def local(
    hidden,
    unembed,
    value_proj,
    output_proj,
    norm_gains,
    survive,
    lengths,
    assign,
    advantage,
    reference_logit,
    recorded_gap,
):
    resp_count = hidden.shape[0]
    positions = hidden.shape[1]
    model_width = hidden.shape[2]
    half_value = value_proj.shape[2]
    micro_count = resp_count // MB_RESP
    row_count = MB_RESP * positions
    section_count = lax.axis_size("section")
    section_index = lax.axis_index("section")
    is_last = section_index == section_count - 1
    norm_gain = norm_gains[0]
    alive_mask = jnp.repeat(survive, GROUP)
    local_count = jnp.sum((alive_mask * lengths).astype(jnp.float32))
    gathered_value, gathered_output = turned_gather((value_proj, output_proj), "dp", (1, 2))
    w_first = gathered_value[0]
    w_second = gathered_output[0]

    def pick(array):
        return jnp.take(array, assign, axis=0, mode="fill", fill_value=0)

    slot_hidden = pick(hidden).reshape(micro_count, row_count, model_width)
    slot_unembed = pick(unembed).reshape(micro_count, row_count, model_width)
    position_index = lax.broadcasted_iota(jnp.int32, (resp_count, positions), 1)
    live_mask = (position_index < pick(lengths)[:, None]).astype(jnp.float32)
    advantages = jnp.broadcast_to(pick(advantage)[:, None], (resp_count, positions))
    gap_rows = pick(recorded_gap)
    clipped = (advantages > 0) & (gap_rows > clip_high) | (advantages < 0) & (gap_rows < clip_low)
    kept_mask = 1.0 - clipped.astype(jnp.float32)
    weight_rows = (-loss_scale * advantages * kept_mask * live_mask).reshape(micro_count, row_count)
    logit_base = pick(reference_logit).reshape(micro_count, row_count)
    step_count = micro_count + section_count - 1
    store_in = jnp.zeros((micro_count, row_count, model_width), jnp.bfloat16)
    store_normed = jnp.zeros((micro_count, row_count, model_width), jnp.bfloat16)
    store_projected = jnp.zeros((micro_count, row_count, half_value), jnp.bfloat16)
    store_out = jnp.zeros((micro_count, row_count, model_width), jnp.bfloat16)
    arriving = jnp.zeros((row_count, model_width), jnp.bfloat16)
    for step_index in range(step_count):
        micro_index = step_index - section_index
        active = (micro_index >= 0) & (micro_index < micro_count)
        clamped = jnp.clip(micro_index, 0, micro_count - 1)
        entering = jnp.where(section_index == 0, take_slot(slot_hidden, clamped), arriving)
        values, inverse, normed = norm_forward(entering, norm_gain)
        projected = jnp.dot(normed, w_first, preferred_element_type=jnp.float32).astype(
            jnp.bfloat16
        )
        partial_out = jnp.dot(projected, w_second, preferred_element_type=jnp.float32)
        mixed_sum = taken_together(partial_out.astype(jnp.bfloat16), "tensor").astype(jnp.float32)
        leaving = (values + mixed_sum).astype(jnp.bfloat16)
        store_in = put_slot(store_in, entering, clamped, active)
        store_normed = put_slot(store_normed, normed, clamped, active)
        store_projected = put_slot(store_projected, projected, clamped, active)
        store_out = put_slot(store_out, leaving, clamped, active)
        arriving = from_behind(leaving, "section", 1)
    store_upstream = jnp.zeros((micro_count, row_count, model_width), jnp.bfloat16)
    store_grad_value = jnp.zeros((micro_count, row_count, half_value), jnp.bfloat16)
    arriving = jnp.zeros((row_count, model_width), jnp.bfloat16)
    for step_index in range(step_count):
        micro_index = step_index - (section_count - 1 - section_index)
        active = (micro_index >= 0) & (micro_index < micro_count)
        clamped = jnp.clip(micro_index, 0, micro_count - 1)
        top_rows = take_slot(store_out, clamped).astype(jnp.float32)
        unembed_rows = take_slot(slot_unembed, clamped).astype(jnp.float32)
        logit = jnp.sum(top_rows * unembed_rows, axis=-1)
        seed_rows = take_slot(weight_rows, clamped) * jnp.exp(
            logit - take_slot(logit_base, clamped)
        )
        start_grad = (seed_rows[:, None] * unembed_rows).astype(jnp.bfloat16)
        upstream = jnp.where(is_last, start_grad, arriving)
        entering = take_slot(store_in, clamped)
        normed = take_slot(store_normed, clamped)
        projected = take_slot(store_projected, clamped)
        grad_projected = contract_last(upstream, w_second).astype(jnp.bfloat16)
        partial_norm = contract_last(grad_projected, w_first)
        grad_normed = taken_together(partial_norm.astype(jnp.bfloat16), "tensor").astype(
            jnp.float32
        )
        values, inverse, unused_normed = norm_forward(entering, norm_gain)
        grad_entering = (
            upstream.astype(jnp.float32) + norm_backward(values, inverse, norm_gain, grad_normed)
        ).astype(jnp.bfloat16)
        store_upstream = put_slot(store_upstream, upstream, clamped, active)
        store_grad_value = put_slot(store_grad_value, grad_projected, clamped, active)
        arriving = from_behind(grad_entering, "section", -1)
    flat_normed = store_normed.reshape(micro_count * row_count, model_width)
    flat_upstream = store_upstream.reshape(micro_count * row_count, model_width)
    flat_grad_value = store_grad_value.reshape(micro_count * row_count, half_value)
    flat_projected = store_projected.reshape(micro_count * row_count, half_value)
    reduced = lax.psum_scatter(
        jnp.concatenate(
            [
                contract_first(flat_normed, flat_grad_value),
                contract_first(flat_upstream, flat_projected),
            ],
            axis=1,
        ).astype(jnp.bfloat16),
        "dp",
        scatter_dimension=0,
        tiled=True,
    ).astype(jnp.float32)
    token_total = of_everyone(local_count, "dp")
    scaled_grads = reduced / token_total
    grad_value = scaled_grads[:, :half_value][None]
    grad_output = scaled_grads[:, half_value:].T[None]
    return (grad_value, grad_output)


def solution(mesh):
    placed = (
        P(("groups", "dp"), None, None),
        P(("groups", "dp"), None, None),
        P("section", "dp", "tensor"),
        P("section", "tensor", "dp"),
        P("section", None),
        P(("groups", "dp")),
        P(("groups", "dp")),
        P(("groups", "dp")),
        P(("groups", "dp")),
        P(("groups", "dp"), None),
        P(("groups", "dp"), None),
    )
    return jax.shard_map(
        local,
        mesh=mesh,
        in_specs=placed,
        out_specs=(
            P(("groups", "section"), "dp", "tensor"),
            P(("groups", "section"), "tensor", "dp"),
        ),
        check_vma=False,
    )
```

profile of v0, /device:TPU:40, one launch (start us, length us, event | category | flops | bytes accessed | tf_op | source)
XLA Modules:
  0.0 453.6 jit_solution(10710032838537592977)
XLA Ops:
  7.3 1.8 pad_maximum_fusion.1
  11.3 3.1 gather_fusion.4
  16.6 2.7 broadcast_select_fusion.1
  20.5 82.2 %all-gather.2.cloned.1.call-done = bf16[5120,512]{1,0:T(8,128)(2,1)} async-done(((bf16[320,512]{1,0:T(8,128)(2,1)}), bf16[5120,512]{1,0:T(8,128)(2,1)}) %all-gather.2.cloned.1.call-update) | async-done | bytes 5242896 | tf_op jit(solution)/shard_map/all_gather | solution.py:22
  102.7 2.6 bitcast_dynamic-update-slice_fusion.19
  105.3 2.6 convolution_convert_fusion.8
  108.1 4.9 %all_to_all.51 = bf16[2,64,5120]{2,1,0:T(8,128)(2,1)S(1)} all-to-all(bf16[2,64,5120]{2,1,0:T(8,128)(2,1)S(1)} %broadcast_in_dim.204), channel_id=1, replica_groups=mesh['groups'=2,'dp'=16,'section'=4,'tensor'=2] {'tensor'}, dimensions={0} | all-to-all | bytes 2621440 | tf_op jit(solution)/shard_map/all_to_all | solution.py:34
  113.5 3.7 collective-permute-start
  117.3 14.1 %collective-permute-done = bf16[64,5120]{1,0:T(8,128)(2,1)S(1)} collective-permute-done((bf16[64,5120]{1,0:T(8,128)(2,1)S(1)}, bf16[64,5120]{1,0:T(8,128)(2,1)S(1)}, u32[]{:S(2)}, u32[]{:S(2)}) %collective-permute-start) | collective-permute-done | bytes 655392 | tf_op jit(solution)/shard_map/ppermute | solution.py:46
  133.7 0.9 convolution_convert_fusion.7
  134.6 1.2 broadcast_in_dim.206
  135.8 4.5 %all-to-all-start.1 = ((bf16[2,64,5120]{2,1,0:T(8,128)(2,1)}), bf16[2,64,5120]{2,1,0:T(8,128)(2,1)}, u32[]{:S(2)}, u32[]{:S(2)}) async-start(bf16[2,64,5120]{2,1,0:T(8,128)(2,1)} %broadcast_in_dim.206), calls=%async_computation.1 | async-start | bytes 2621440 | tf_op jit(solution)/shard_map/all_to_all | solution.py:34
  140.3 1.2 constant_dynamic-slice_fusion.28
  141.6 1.2 all-to-all-done.1
  142.7 1.8 convert_reduce_fusion.7
  144.9 4.7 %collective-permute-start.1 = (bf16[64,5120]{1,0:T(8,128)(2,1)S(1)}, bf16[64,5120]{1,0:T(8,128)(2,1)S(1)}, u32[]{:S(2)}, u32[]{:S(2)}) collective-permute-start(bf16[64,5120]{1,0:T(8,128)(2,1)S(1)} %get-tuple-element.43), channel_id=1, source_target_pairs={{0,2},{2,4},{4,6},{1,3},{3,5},{5,7},{8,10},{10,12},{12,14},{9,11},... | collective-permute-start | bytes 1966088 | tf_op jit(solution)/shard_map/ppermute | solution.py:46
  149.8 14.1 %collective-permute-done.1 = bf16[64,5120]{1,0:T(8,128)(2,1)S(1)} collective-permute-done((bf16[64,5120]{1,0:T(8,128)(2,1)S(1)}, bf16[64,5120]{1,0:T(8,128)(2,1)S(1)}, u32[]{:S(2)}, u32[]{:S(2)}) %collective-permute-start.1) | collective-permute-done | bytes 655392 | tf_op jit(solution)/shard_map/ppermute | solution.py:46
  165.1 0.9 convolution_convert_fusion.6
  166.2 4.8 %all_to_all.52 = bf16[2,64,5120]{2,1,0:T(8,128)(2,1)S(1)} all-to-all(bf16[2,64,5120]{2,1,0:T(8,128)(2,1)S(1)} %broadcast_in_dim.208), channel_id=1, replica_groups=mesh['groups'=2,'dp'=16,'section'=4,'tensor'=2] {'tensor'}, dimensions={0} | all-to-all | bytes 2621440 | tf_op jit(solution)/shard_map/all_to_all | solution.py:34
  171.5 4.5 collective-permute-start.2
  176.1 14.1 %collective-permute-done.2 = bf16[64,5120]{1,0:T(8,128)(2,1)S(1)} collective-permute-done((bf16[64,5120]{1,0:T(8,128)(2,1)S(1)}, bf16[64,5120]{1,0:T(8,128)(2,1)S(1)}, u32[]{:S(2)}, u32[]{:S(2)}) %collective-permute-start.2) | collective-permute-done | bytes 655392 | tf_op jit(solution)/shard_map/ppermute | solution.py:46
  191.4 0.9 convolution_convert_fusion.5
  192.5 4.8 %all_to_all.53 = bf16[2,64,5120]{2,1,0:T(8,128)(2,1)S(1)} all-to-all(bf16[2,64,5120]{2,1,0:T(8,128)(2,1)S(1)} %broadcast_in_dim.210), channel_id=1, replica_groups=mesh['groups'=2,'dp'=16,'section'=4,'tensor'=2] {'tensor'}, dimensions={0} | all-to-all | bytes 2621440 | tf_op jit(solution)/shard_map/all_to_all | solution.py:34
  197.8 4.6 %collective-permute-start.3 = (bf16[64,5120]{1,0:T(8,128)(2,1)S(1)}, bf16[64,5120]{1,0:T(8,128)(2,1)S(1)}, u32[]{:S(2)}, u32[]{:S(2)}) collective-permute-start(bf16[64,5120]{1,0:T(8,128)(2,1)S(1)} %get-tuple-element.39), channel_id=1, source_target_pairs={{0,2},{2,4},{4,6},{1,3},{3,5},{5,7},{8,10},{10,12},{12,14},{9,11},... | collective-permute-start | bytes 1966088 | tf_op jit(solution)/shard_map/ppermute | solution.py:46
  202.6 0.9 constant_dynamic-slice_fusion.25
  203.5 13.0 %collective-permute-done.3 = bf16[64,5120]{1,0:T(8,128)(2,1)S(1)} collective-permute-done((bf16[64,5120]{1,0:T(8,128)(2,1)S(1)}, bf16[64,5120]{1,0:T(8,128)(2,1)S(1)}, u32[]{:S(2)}, u32[]{:S(2)}) %collective-permute-start.3) | collective-permute-done | bytes 655392 | tf_op jit(solution)/shard_map/ppermute | solution.py:46
  216.5 1.2 broadcast.283.clone.2
  217.8 1.4 bitcast_dynamic-update-slice_fusion.4
  220.5 0.9 convolution_convert_fusion.4
  221.4 1.2 broadcast_in_dim.219
  222.6 4.6 %all-to-all-start.4 = ((bf16[2,64,5120]{2,1,0:T(8,128)(2,1)}), bf16[2,64,5120]{2,1,0:T(8,128)(2,1)}, u32[]{:S(2)}, u32[]{:S(2)}) async-start(bf16[2,64,5120]{2,1,0:T(8,128)(2,1)} %broadcast_in_dim.219), calls=%async_computation.4 | async-start | bytes 2621440 | tf_op jit(solution)/shard_map/all_to_all | solution.py:34
  227.2 1.1 constant_dynamic-slice_fusion.33
  228.4 1.1 bitcast_dynamic-update-slice_fusion.14
  229.5 1.1 constant_dynamic-slice_fusion.32
  230.7 1.1 bitcast_dynamic-update-slice_fusion.13
  231.8 1.1 constant_dynamic-slice_fusion.31
  233.0 1.1 bitcast_dynamic-update-slice_fusion.12
  234.1 2.1 constant_dynamic-slice_fusion.30
  236.2 1.8 convert_reduce_fusion.4
  238.1 2.6 bitcast_dynamic-update-slice_fusion.11
  240.7 0.9 fusion.16
  242.4 0.9 convolution_convert_fusion.3
  243.4 4.8 %all_to_all.54 = bf16[2,64,5120]{2,1,0:T(8,128)(2,1)S(1)} all-to-all(bf16[2,64,5120]{2,1,0:T(8,128)(2,1)S(1)} %broadcast_in_dim.226), channel_id=1, replica_groups=mesh['groups'=2,'dp'=16,'section'=4,'tensor'=2] {'tensor'}, dimensions={0} | all-to-all | bytes 2621440 | tf_op jit(solution)/shard_map/all_to_all | solution.py:34
  248.4 1.1 copy-done.7
  250.8 1.3 collective-permute-start.4
  252.7 17.6 %collective-permute-done.4 = bf16[64,5120]{1,0:T(8,128)(2,1)S(1)} collective-permute-done((bf16[64,5120]{1,0:T(8,128)(2,1)S(1)}, bf16[64,5120]{1,0:T(8,128)(2,1)S(1)}, u32[]{:S(2)}, u32[]{:S(2)}) %collective-permute-start.4) | collective-permute-done | bytes 655392 | tf_op jit(solution)/shard_map/ppermute | solution.py:46
  271.3 0.9 convolution_convert_fusion.2
  272.3 4.8 %all_to_all.55 = bf16[2,64,5120]{2,1,0:T(8,128)(2,1)S(1)} all-to-all(bf16[2,64,5120]{2,1,0:T(8,128)(2,1)S(1)} %broadcast_in_dim.228), channel_id=1, replica_groups=mesh['groups'=2,'dp'=16,'section'=4,'tensor'=2] {'tensor'}, dimensions={0} | all-to-all | bytes 2621440 | tf_op jit(solution)/shard_map/all_to_all | solution.py:34
  278.1 1.5 collective-permute-start.5
  279.7 17.1 %collective-permute-done.5 = bf16[64,5120]{1,0:T(8,128)(2,1)S(1)} collective-permute-done((bf16[64,5120]{1,0:T(8,128)(2,1)S(1)}, bf16[64,5120]{1,0:T(8,128)(2,1)S(1)}, u32[]{:S(2)}, u32[]{:S(2)}) %collective-permute-start.5) | collective-permute-done | bytes 655392 | tf_op jit(solution)/shard_map/ppermute | solution.py:46
  297.8 0.9 convolution_convert_fusion.1
  298.8 4.8 %all_to_all.56 = bf16[2,64,5120]{2,1,0:T(8,128)(2,1)S(1)} all-to-all(bf16[2,64,5120]{2,1,0:T(8,128)(2,1)S(1)} %broadcast_in_dim.230), channel_id=1, replica_groups=mesh['groups'=2,'dp'=16,'section'=4,'tensor'=2] {'tensor'}, dimensions={0} | all-to-all | bytes 2621440 | tf_op jit(solution)/shard_map/all_to_all | solution.py:34
  304.6 1.3 collective-permute-start.6
  306.0 17.3 %collective-permute-done.6 = bf16[64,5120]{1,0:T(8,128)(2,1)S(1)} collective-permute-done((bf16[64,5120]{1,0:T(8,128)(2,1)S(1)}, bf16[64,5120]{1,0:T(8,128)(2,1)S(1)}, u32[]{:S(2)}, u32[]{:S(2)}) %collective-permute-start.6) | collective-permute-done | bytes 655392 | tf_op jit(solution)/shard_map/ppermute | solution.py:46
  324.3 0.9 convolution_convert_fusion
  325.3 4.8 %all_to_all.57 = bf16[2,64,5120]{2,1,0:T(8,128)(2,1)S(1)} all-to-all(bf16[2,64,5120]{2,1,0:T(8,128)(2,1)S(1)} %broadcast_in_dim.232), channel_id=1, replica_groups=mesh['groups'=2,'dp'=16,'section'=4,'tensor'=2] {'tensor'}, dimensions={0} | all-to-all | bytes 2621440 | tf_op jit(solution)/shard_map/all_to_all | solution.py:34
  331.1 1.3 collective-permute-start.7
  332.5 17.3 %collective-permute-done.7 = bf16[64,5120]{1,0:T(8,128)(2,1)S(1)} collective-permute-done((bf16[64,5120]{1,0:T(8,128)(2,1)S(1)}, bf16[64,5120]{1,0:T(8,128)(2,1)S(1)}, u32[]{:S(2)}, u32[]{:S(2)}) %collective-permute-start.7) | collective-permute-done | bytes 655392 | tf_op jit(solution)/shard_map/ppermute | solution.py:46
  350.5 2.2 fusion
  354.0 2.7 pad_maximum_fusion
  356.7 7.9 %copy.34 = bf16[5120,512]{1,0:T(8,128)(2,1)} copy(bf16[5120,512]{0,1:T(8,128)(2,1)} %pad_maximum_fusion) | data formatting | bytes 10485760
  366.6 19.4 %all_to_all.58 = f32[16,1,1]{2,1,0:T(1,128)S(1)} all-to-all(f32[16,1,1]{2,1,0:T(1,128)S(1)} %broadcast_in_dim.243), channel_id=1, replica_groups=mesh['groups'=2,'dp'=16,'section'=4,'tensor'=2] {'dp'}, dimensions={0} | all-to-all | bytes 128 | tf_op jit(solution)/shard_map/all_to_all | solution.py:34
  386.6 56.2 %reduce-scatter.4.cloned.1.call-done = bf16[320,512]{1,0:T(8,128)(2,1)} async-done(((bf16[5120,512]{1,0:T(8,128)(2,1)}), bf16[320,512]{1,0:T(8,128)(2,1)}) %reduce-scatter.4.cloned.1.call-update) | async-done | bytes 327696
  442.9 1.2 copy.35
  (178 shorter events, 29.7 us)
Async XLA Ops:
  7.2 3.4 copy-start
  7.2 2.7 copy-start.2
  7.2 95.5 %all-gather.2.cloned.1.call-start = ((), (), s32[]{:S(2)}) async-start(), calls=%async_computation.11 | async-start | bytes 5570560 | tf_op jit(solution)/shard_map/all_gather | solution.py:22
  11.2 3.1 copy-start.3
  11.2 3.8 copy-start.22
  11.2 4.4 copy-start.23
  11.2 5.0 %copy-start.24 = (s32[16]{0:T(128)S(1)}, s32[16]{0:T(128)}, u32[]{:S(2)}) copy-start(s32[16]{0:T(128)} %param.22) | copy-start | bytes 196
  19.3 1.1 copy-start.13
  19.5 83.2 %copy-start.20 = (f32[1,5120]{1,0:T(1,128)S(1)}, f32[1,5120]{1,0:T(1,128)}, u32[]{:S(2)}) copy-start(f32[1,5120]{1,0:T(1,128)} %param.19) | copy-start | bytes 61444
  108.1 5.2 %copy-start.14 = (bf16[16,8,5120]{2,1,0:T(8,128)(2,1)S(1)}, bf16[16,8,5120]{2,1,0:T(8,128)(2,1)}, u32[]{:S(2)}) copy-start(bf16[16,8,5120]{2,1,0:T(8,128)(2,1)} %copy-done.13) | copy-start | bytes 3932164
  113.0 19.3 %slice-start = ((s8[5242880]{0:T(1024)(128)(4,1)}), s8[4194304]{0:T(1024)(128)(4,1)S(1)}, s32[]{:S(2)}) async-start(s8[5242880]{0:T(1024)(128)(4,1)} %bitcast.385), calls=%async_computation.13 | async-start | bytes 8388608
  113.5 18.0 %collective-permute-start = (bf16[64,5120]{1,0:T(8,128)(2,1)S(1)}, bf16[64,5120]{1,0:T(8,128)(2,1)S(1)}, u32[]{:S(2)}, u32[]{:S(2)}) collective-permute-start(bf16[64,5120]{1,0:T(8,128)(2,1)S(1)} %fusion.21), channel_id=1, source_target_pairs={{0,2},{2,4},{4,6},{1,3},{3,5},{5,7},{8,10},{10,12},{12,14},{9,11},... | collective-permute-start | bytes 1966088 | tf_op jit(solution)/shard_map/ppermute | solution.py:46
  117.3 15.1 %slice-start.1 = ((s8[5242880]{0:T(1024)(128)(4,1)}), s8[1048576]{0:T(1024)(128)(4,1)S(1)}, s32[]{:S(2)}) async-start(s8[5242880]{0:T(1024)(128)(4,1)} %bitcast.385), calls=%async_computation.14 | async-start | bytes 2097152
  132.1 1.1 copy-start.4
  132.1 1.6 copy-start.9
  135.8 7.0 %all-to-all-start.1 = ((bf16[2,64,5120]{2,1,0:T(8,128)(2,1)}), bf16[2,64,5120]{2,1,0:T(8,128)(2,1)}, u32[]{:S(2)}, u32[]{:S(2)}) async-start(bf16[2,64,5120]{2,1,0:T(8,128)(2,1)} %broadcast_in_dim.206), calls=%async_computation.1 | async-start | bytes 2621440 | tf_op jit(solution)/shard_map/all_to_all | solution.py:34
  140.3 24.1 %slice-start.2 = ((s8[5242880]{0:T(1024)(128)(4,1)}), s8[1048576]{0:T(1024)(128)(4,1)S(1)}, s32[]{:S(2)}) async-start(s8[5242880]{0:T(1024)(128)(4,1)} %bitcast.387), calls=%async_computation.15 | async-start | bytes 2097152
  142.7 1.8 copy-start.10
  142.7 6.9 %copy-start.5 = (bf16[2,64,5120]{2,1,0:T(8,128)(2,1)S(1)}, bf16[2,64,5120]{2,1,0:T(8,128)(2,1)}, u32[]{:S(2)}) copy-start(bf16[2,64,5120]{2,1,0:T(8,128)(2,1)} %copy-done.4) | copy-start | bytes 3932164
  144.6 19.9 %slice-start.3 = ((s8[5242880]{0:T(1024)(128)(4,1)}), s8[4194304]{0:T(1024)(128)(4,1)S(1)}, s32[]{:S(2)}) async-start(s8[5242880]{0:T(1024)(128)(4,1)} %bitcast.387), calls=%async_computation.16 | async-start | bytes 8388608
  144.9 19.0 %collective-permute-start.1 = (bf16[64,5120]{1,0:T(8,128)(2,1)S(1)}, bf16[64,5120]{1,0:T(8,128)(2,1)S(1)}, u32[]{:S(2)}, u32[]{:S(2)}) collective-permute-start(bf16[64,5120]{1,0:T(8,128)(2,1)S(1)} %get-tuple-element.43), channel_id=1, source_target_pairs={{0,2},{2,4},{4,6},{1,3},{3,5},{5,7},{8,10},{10,12},{12,14},{9,11},... | collective-permute-start | bytes 1966088 | tf_op jit(solution)/shard_map/ppermute | solution.py:46
  149.7 14.2 %copy-start.15 = (bf16[16,8,5120]{2,1,0:T(8,128)(2,1)S(1)}, bf16[16,8,5120]{2,1,0:T(8,128)(2,1)}, u32[]{:S(2)}) copy-start(bf16[16,8,5120]{2,1,0:T(8,128)(2,1)} %copy-done.13) | copy-start | bytes 3932164
  171.5 18.7 %collective-permute-start.2 = (bf16[64,5120]{1,0:T(8,128)(2,1)S(1)}, bf16[64,5120]{1,0:T(8,128)(2,1)S(1)}, u32[]{:S(2)}, u32[]{:S(2)}) collective-permute-start(bf16[64,5120]{1,0:T(8,128)(2,1)S(1)} %get-tuple-element.41), channel_id=1, source_target_pairs={{0,2},{2,4},{4,6},{1,3},{3,5},{5,7},{8,10},{10,12},{12,14},{9,11},... | collective-permute-start | bytes 1966088 | tf_op jit(solution)/shard_map/ppermute | solution.py:46
  190.5 7.0 %copy-start.16 = (bf16[64,5120]{1,0:T(8,128)(2,1)}, bf16[64,5120]{1,0:T(8,128)(2,1)S(1)}, u32[]{:S(2)}) copy-start(bf16[64,5120]{1,0:T(8,128)(2,1)S(1)} %get-tuple-element.33) | copy-start | bytes 1966084
  197.8 5.7 %copy-start.11 = (bf16[2,64,5120]{2,1,0:T(8,128)(2,1)}, bf16[2,64,5120]{2,1,0:T(8,128)(2,1)S(1)}, u32[]{:S(2)}) copy-start(bf16[2,64,5120]{2,1,0:T(8,128)(2,1)S(1)} %get-tuple-element.38) | copy-start | bytes 3932164
  197.8 18.7 %collective-permute-start.3 = (bf16[64,5120]{1,0:T(8,128)(2,1)S(1)}, bf16[64,5120]{1,0:T(8,128)(2,1)S(1)}, u32[]{:S(2)}, u32[]{:S(2)}) collective-permute-start(bf16[64,5120]{1,0:T(8,128)(2,1)S(1)} %get-tuple-element.39), channel_id=1, source_target_pairs={{0,2},{2,4},{4,6},{1,3},{3,5},{5,7},{8,10},{10,12},{12,14},{9,11},... | collective-permute-start | bytes 1966088 | tf_op jit(solution)/shard_map/ppermute | solution.py:46
  219.2 1.1 copy-start.6
  219.2 1.3 copy-start.18
  222.6 13.6 %all-to-all-start.4 = ((bf16[2,64,5120]{2,1,0:T(8,128)(2,1)}), bf16[2,64,5120]{2,1,0:T(8,128)(2,1)}, u32[]{:S(2)}, u32[]{:S(2)}) async-start(bf16[2,64,5120]{2,1,0:T(8,128)(2,1)} %broadcast_in_dim.219), calls=%async_computation.4 | async-start | bytes 2621440 | tf_op jit(solution)/shard_map/all_to_all | solution.py:34
  227.2 215.7 %reduce-scatter.4.cloned.1.call-start = ((), (), s32[]{:S(2)}) async-start(), calls=%async_computation.12 | async-start | bytes 5570560
  230.6 2.3 copy-start.17
  233.0 5.1 %copy-start.21 = (bf16[1,64,5120]{2,1,0:T(8,128)(2,1)S(1)}, bf16[1,64,5120]{2,1,0:T(8,128)(2,1)}, u32[]{:S(2)}) copy-start(bf16[1,64,5120]{2,1,0:T(8,128)(2,1)} %constant_dynamic-slice_fusion.25) | copy-start | bytes 1966084
  234.1 4.0 copy-start.12
  236.2 1.9 copy-start.19
  236.2 5.5 %slice-start.4 = ((s8[5242880]{0:T(1024)(128)(4,1)}), s8[4194304]{0:T(1024)(128)(4,1)S(1)}, s32[]{:S(2)}) async-start(s8[5242880]{0:T(1024)(128)(4,1)} %bitcast.389), calls=%async_computation.17 | async-start | bytes 8388608
  238.1 2.6 copy-start.8
  238.1 3.6 slice-start.5
  248.2 1.3 copy-start.7
  250.8 19.5 %collective-permute-start.4 = (bf16[64,5120]{1,0:T(8,128)(2,1)S(1)}, bf16[64,5120]{1,0:T(8,128)(2,1)S(1)}, u32[]{:S(2)}, u32[]{:S(2)}) collective-permute-start(bf16[64,5120]{1,0:T(8,128)(2,1)S(1)} %fusion.45), channel_id=1, source_target_pairs={{2,0},{4,2},{6,4},{3,1},{5,3},{7,5},{10,8},{12,10},{14,12},{11,9},... | collective-permute-start | bytes 1966088 | tf_op jit(solution)/shard_map/ppermute | solution.py:46
  278.1 18.7 %collective-permute-start.5 = (bf16[64,5120]{1,0:T(8,128)(2,1)S(1)}, bf16[64,5120]{1,0:T(8,128)(2,1)S(1)}, u32[]{:S(2)}, u32[]{:S(2)}) collective-permute-start(bf16[64,5120]{1,0:T(8,128)(2,1)S(1)} %fusion.51), channel_id=1, source_target_pairs={{2,0},{4,2},{6,4},{3,1},{5,3},{7,5},{10,8},{12,10},{14,12},{11,9},... | collective-permute-start | bytes 1966088 | tf_op jit(solution)/shard_map/ppermute | solution.py:46
  304.6 18.7 %collective-permute-start.6 = (bf16[64,5120]{1,0:T(8,128)(2,1)S(1)}, bf16[64,5120]{1,0:T(8,128)(2,1)S(1)}, u32[]{:S(2)}, u32[]{:S(2)}) collective-permute-start(bf16[64,5120]{1,0:T(8,128)(2,1)S(1)} %fusion.57), channel_id=1, source_target_pairs={{2,0},{4,2},{6,4},{3,1},{5,3},{7,5},{10,8},{12,10},{14,12},{11,9},... | collective-permute-start | bytes 1966088 | tf_op jit(solution)/shard_map/ppermute | solution.py:46
  331.1 18.7 %collective-permute-start.7 = (bf16[64,5120]{1,0:T(8,128)(2,1)S(1)}, bf16[64,5120]{1,0:T(8,128)(2,1)S(1)}, u32[]{:S(2)}, u32[]{:S(2)}) collective-permute-start(bf16[64,5120]{1,0:T(8,128)(2,1)S(1)} %fusion.63), channel_id=1, source_target_pairs={{2,0},{4,2},{6,4},{3,1},{5,3},{7,5},{10,8},{12,10},{14,12},{11,9},... | collective-permute-start | bytes 1966088 | tf_op jit(solution)/shard_map/ppermute | solution.py:46
  444.1 2.6 copy-start.1
Sparse Core Ops, SparseCore 0:
  10.4 92.2 all-gather.1
  364.9 77.9 reduce-scatter.3
where the time goes:
time: 456 us; the launch traced here: 454 us
  waiting for transfers between devices  264 us (58%)
  blocking collectives  53.1 us (12%)
  local copies, waits for them, and re-layouts  34.1 us (7%)
  other arithmetic  33 us (7%)
  starting transfers between devices  32.2 us (7%)
  matrix products  20.9 us (5%)
  between operations  15.8 us (3%)
    ppermute x8, waiting for transfers between devices, from_behind(): return lax.ppermute(block, axis, route)  125 us
    all_gather x1, waiting for transfers between devices, turned_gather(): result = lax.all_gather(both, axis, axis=0, tiled=True)  82.2 us
    unnamed x3, waiting for transfers between devices  56.3 us
    all_to_all x8, blocking collectives, copy_for_each(): lax.all_to_all(jnp.broadcast_to(array[None], (devices, *array.shape)), ax...  53.1 us
    ppermute x8, starting transfers between devices, from_behind(): return lax.ppermute(block, axis, route)  23 us
    unnamed x68, local copies, waits for them, and re-layouts  13.9 us
    dynamic_update_slice x17, other arithmetic, put_slot(): lax.dynamic_update_index_in_dim(slot_store, jnp.where(active, new_value,...  11.7 us
    all_to_all x2, starting transfers between devices, copy_for_each(): lax.all_to_all(jnp.broadcast_to(array[None], (devices, *array.shape)), ax...  9.13 us
  transfers between devices with their start and end apart: 12, of which 11 were waited for; matrix products, arithmetic and copies ran while one was open for 5% of the time, Pallas kernels for 0%

commit v1 on v0

v1 whole, which is shorter than its diff:
```python
import functools
import math

import jax
import jax.numpy as jnp
from jax import lax
from jax.experimental import pallas as pl
from jax.experimental.pallas import tpu as pltpu
from jax.sharding import PartitionSpec as P

GROUP = 16

eps_norm = 1e-06
loss_scale = 4096.0
clip_high = math.log(1.28)
clip_low = math.log(0.8)

F32 = jnp.float32
BF16 = jnp.bfloat16
MESH = pl.DeviceIdType.MESH


def dot_nn(a, b):
    return jnp.dot(a, b, preferred_element_type=F32)


def dot_nt(a, b):
    return lax.dot_general(a, b, (((1,), (1,)), ((), ())), preferred_element_type=F32)


def dot_tn(a, b):
    return lax.dot_general(a, b, (((0,), (0,)), ((), ())), preferred_element_type=F32)


def kernel(
    dims,
    hid, une, wown, gown, rowd, tgt,
    out,
    wfull, gall, cnts, xs, us, projs, rcols, gcur, wg, rbu, rbd, obuf, osrc,
    arsrc, arbuf, stsrc, stbuf, dsrc, dbuf, tsrc, tbuf,
    xa_s, xa_r, ga_s, ga_r, ag_s, ag_r, cn_s, cn_r, ar_s, ar_r, st_s, st_r,
    d_s, d_r, t_s, t_r, rs_s, rs_r, o_s, o_r,
):
    n, ns, rows, sub, half, width = dims
    q = n * sub
    layers = ns
    j = lax.axis_index("dp")
    s = lax.axis_index("section")
    t = lax.axis_index("tensor")
    up, down, other = lax.rem(j + 1, n), lax.rem(j + n - 1, n), 1 - t
    pending = []

    def remote(src, dst, send, recv, device):
        return pltpu.make_async_remote_copy(
            src_ref=src, dst_ref=dst, send_sem=send, recv_sem=recv,
            device_id=device, device_id_type=MESH,
        )

    def go(*args):
        copy = remote(*args)
        copy.start()
        pending.append(copy)
        return copy

    def block(offset):
        return lax.rem(j + n + offset, n)

    barrier = pltpu.get_barrier_semaphore()
    peers = [{"dp": up}, {"dp": down}, {"tensor": other}]
    peers += [{"section": lax.rem(s + k, ns)} for k in range(1, ns)]
    for peer in peers:
        pl.semaphore_signal(barrier, inc=1, device_id=peer, device_id_type=MESH)
    pl.semaphore_wait(barrier, len(peers))

    for k in range(1, ns):
        to = lax.rem(s + k, ns)
        go(wown.at[to], wfull.at[s, j], xa_s.at[k - 1], xa_r.at[s], {"section": to})
        go(gown.at[to], gall.at[s], ga_s.at[k - 1], ga_r.at[s], {"section": to})
    wfull[s, j] = wown[s]
    gall[s] = gown[s]
    cnts[j] = jnp.broadcast_to(rowd[3:4, :], cnts.shape[1:])

    def layer_arrived(l):
        @pl.when(s != l)
        def _():
            away = {"section": lax.rem(s + 1, ns)}
            remote(wown.at[0], wfull.at[l, j], xa_s.at[0], xa_r.at[l], away).wait_recv()
            remote(gown.at[0], gall.at[l], ga_s.at[0], ga_r.at[l], away).wait_recv()

    steps = n // 2

    def reach(l, way):
        return steps if (l + way) % 2 == 0 else steps - 1

    toward = [{"dp": up}, {"dp": down}]
    sign = [1, -1]

    def ag_send(l, k, way):
        if k <= reach(l, way):
            b = block(-sign[way] * (k - 1))
            go(wfull.at[l, b], wfull.at[l, b], ag_s.at[l, way, k - 1], ag_r.at[l, way, k - 1], toward[way])
            if l == 0:
                go(cnts.at[b], cnts.at[b], cn_s.at[way, k - 1], cn_r.at[way, k - 1], toward[way])

    def ag_recv(l, k, way):
        if k <= reach(l, way):
            b = block(-sign[way] * k)
            remote(wfull.at[l, b], wfull.at[l, b], ag_s.at[l, way, k - 1], ag_r.at[l, way, k - 1], toward[way]).wait_recv()
            if l == 0:
                remote(cnts.at[b], cnts.at[b], cn_s.at[way, k - 1], cn_r.at[way, k - 1], toward[way]).wait_recv()

    def ag_tick(ls, k):
        for l in ls:
            for way in range(2):
                ag_recv(l, k, way)
                ag_send(l, k + 1, way)

    eye = lax.broadcasted_iota(jnp.int32, (rows, rows), 0) == lax.broadcasted_iota(jnp.int32, (rows, rows), 1)

    def to_row(column):
        return jnp.sum(jnp.where(eye, column, 0.0), axis=0, keepdims=True)

    def to_col(row):
        return jnp.sum(jnp.where(eye, row, 0.0), axis=1, keepdims=True)

    def weight(l, first):
        w = wfull[l, :, :, 0:half] if first else wfull[l, :, :, half : 2 * half]
        return w.reshape(q, half)

    def gain(l):
        return jnp.concatenate([gall[l, i : i + 1, :] for i in range(q // 128)], axis=1)

    def ar_send(i, value, stats=None):
        arsrc[i] = value
        if stats is not None:
            first = lax.broadcasted_iota(jnp.int32, (8, rows), 0) == 0
            stsrc[i] = jnp.where(first, stats[0], stats[1])
        for k in range(1, ns):
            to = {"section": lax.rem(s + k, ns)}
            if stats is not None:
                go(stsrc.at[i], stbuf.at[i, k - 1], st_s.at[i, k - 1], st_r.at[i, k - 1], to)
            go(arsrc.at[i], arbuf.at[i, k - 1], ar_s.at[i, k - 1], ar_r.at[i, k - 1], to)

    def ar_recv(i, stats=False):
        away = {"section": lax.rem(s + 1, ns)}
        if stats:
            for k in range(1, ns):
                remote(stsrc.at[i], stbuf.at[i, k - 1], st_s.at[i, k - 1], st_r.at[i, k - 1], away).wait_recv()
            both = stsrc[i]
            for k in range(1, ns):
                both = both + stbuf[i, k - 1]
        for k in range(1, ns):
            remote(arsrc.at[i], arbuf.at[i, k - 1], ar_s.at[i, k - 1], ar_r.at[i, k - 1], away).wait_recv()
        total = arsrc[i].astype(F32)
        for k in range(1, ns):
            total = total + arbuf[i, k - 1].astype(F32)
        return (total, both) if stats else total

    def pair_send(i, value):
        dsrc[i] = value
        go(dsrc.at[i], dbuf.at[i], d_s.at[i], d_r.at[i], {"tensor": other})

    def pair_recv(i):
        remote(dsrc.at[i], dbuf.at[i], d_s.at[i], d_r.at[i], {"tensor": other}).wait_recv()
        return dsrc[i].astype(F32) + dbuf[i].astype(F32)

    def small_send(i, column):
        tsrc[i] = jnp.broadcast_to(to_row(column), (8, rows))
        go(tsrc.at[i], tbuf.at[i], t_s.at[i], t_r.at[i], {"tensor": other})

    def small_recv(i):
        remote(tsrc.at[i], tbuf.at[i], t_s.at[i], t_r.at[i], {"tensor": other}).wait_recv()
        return to_col(tsrc[i, 0:1, :] + tbuf[i, 0:1, :])

    def select_features():
        size = tgt.shape[1]
        place = lax.broadcasted_iota(jnp.int32, (size, size), 0)
        for super_index in range(width // (4 * size)):
            total = None
            for c in range(ns):
                pick = (place + c * size == tgt[0:1, :]).astype(F32).astype(BF16)
                at = (super_index * ns + c) * size
                lhs = jnp.concatenate([hid[:, at : at + size], une[:, at : at + size]], axis=0)
                piece = dot_nn(lhs, pick)
                total = piece if total is None else total + piece
            total = total.astype(BF16)
            xs[0, :, super_index * size : (super_index + 1) * size] = total[:rows]
            us[:, super_index * size : (super_index + 1) * size] = total[rows:]

    def contribute(l):
        x = xs[l].astype(F32)
        xg = (x * gain(l)).astype(BF16)
        partial = dot_nn(xg, weight(l, True)).astype(BF16)
        squares = to_row(jnp.sum(x * x, axis=1, keepdims=True))
        inner = squares
        if l == layers - 1:
            inner = to_row(jnp.sum(x * us[...].astype(F32), axis=1, keepdims=True))
        ar_send(l, partial, (squares, inner))

    def collect(l):
        total, both = ar_recv(l, True)
        inverse = lax.rsqrt(to_col(both[0:1, :]) / width + eps_norm)
        rcols[l] = jnp.broadcast_to(inverse, (rows, 128))
        projs[l] = (total * inverse).astype(BF16)
        return both[1:2, :]

    def mix(l):
        pair_send(l, dot_nt(projs[l], weight(l, False)).astype(BF16))

    def advance(l):
        xs[l + 1] = (xs[l].astype(F32) + pair_recv(l)).astype(BF16)

    def early():
        contribute(0)
        yield
        collect(0)
        mix(0)
        yield
        advance(0)
        contribute(1)
        yield
        collect(1)
        mix(1)
        yield
        advance(1)
        yield

    for l in (0, 1):
        layer_arrived(l)
        for way in range(2):
            ag_send(l, 1, way)
    select_features()
    for k in range(1, steps + 1):
        ag_tick((0, 1), k)
        if k == steps:
            for l in (2, 3):
                layer_arrived(l)
                for way in range(2):
                    ag_send(l, 1, way)
    stage = early()
    for k in range(1, steps + 1):
        next(stage, None)
        ag_tick((2, 3), k)
    for _ in stage:
        pass

    contribute(2)
    ar_send(4, dot_nn(us[...], weight(3, False)).astype(BF16))
    collect(2)
    mix(2)
    advance(2)
    contribute(3)
    inner_row = collect(3)
    top = ar_recv(4)
    small_send(3, jnp.sum(projs[3].astype(F32) * top, axis=1, keepdims=True))

    def wgrad(l, gp):
        normed = (xs[l].astype(F32) * rcols[l, :, 0:1] * gain(l)).astype(BF16)
        wg[l, :, :, 0:half] = dot_tn(normed, gp).astype(BF16).reshape(n, sub, half)
        wg[l, :, :, half : 2 * half] = dot_tn(gcur[...], projs[l]).astype(BF16).reshape(n, sub, half)

    landing = [rbu, rbd]

    def rs_send(l, i, way):
        hops = reach(l, way)
        if i <= hops:
            b = block(sign[way] * (hops - i + 1))
            go(wg.at[l, b], landing[way].at[l, i - 1], rs_s.at[l, way, i - 1], rs_r.at[l, way, i - 1], toward[way])

    def rs_recv(l, i, way):
        hops = reach(l, way)
        if i <= hops:
            b = block(sign[way] * (hops - i))
            remote(wg.at[l, b], landing[way].at[l, i - 1], rs_s.at[l, way, i - 1], rs_r.at[l, way, i - 1], toward[way]).wait_recv()
            wg[l, b] = (wg[l, b].astype(F32) + landing[way][l, i - 1].astype(F32)).astype(BF16)

    position = {}

    def rs_start(l):
        for way in range(2):
            rs_send(l, 1, way)
        position[l] = 1

    def rs_tick():
        for l in sorted(position, reverse=True):
            i = position[l]
            if i > steps:
                continue
            for way in range(2):
                rs_recv(l, i, way)
                rs_send(l, i + 1, way)
            position[l] = i + 1
            if i == steps:
                finish(l)

    def finish(l):
        osrc[l] = wg[l, j]

        @pl.when(s == l)
        def _():
            obuf[l] = osrc[l]

        @pl.when(s != l)
        def _():
            remote(osrc.at[l], obuf.at[s], o_s.at[l], o_r.at[s], {"section": l}).start()

    wcol = to_col(rowd[0:1, :])
    base = to_col(rowd[1:2, :])
    held = to_col(rowd[2:3, :])
    inner = to_col(inner_row)
    logit = inner + small_recv(3)
    seed = wcol * jnp.exp(jnp.where(held > 0.0, logit - base, 0.0))
    gp = (seed * top).astype(BF16)
    gcur[...] = (seed * us[...].astype(F32)).astype(BF16)
    for l in range(layers - 1, 0, -1):
        pair_send(2 + l, dot_nt(gp, weight(l, True)).astype(BF16))
        small_send(l - 1, jnp.sum(gp.astype(F32) * projs[l].astype(F32), axis=1, keepdims=True))
        wgrad(l, gp)
        rs_start(l)
        grad_normed = pair_recv(2 + l)
        inverse = rcols[l, :, 0:1]
        inner = small_recv(l - 1) * (inverse * inverse) / width
        gcur[...] = (
            gcur[...].astype(F32) + inverse * gain(l) * grad_normed - xs[l].astype(F32) * inner
        ).astype(BF16)
        ar_send(4 + l, dot_nn(gcur[...], weight(l - 1, False)).astype(BF16))
        rs_tick()
        gp = ar_recv(4 + l).astype(BF16)
    wgrad(0, gp)
    rs_start(0)
    while any(i <= steps for i in position.values()):
        rs_tick()

    for l in range(layers):
        @pl.when(s != l)
        def _():
            remote(osrc.at[l], obuf.at[l], o_s.at[l], o_r.at[l], {"section": l}).wait_send()
            remote(osrc.at[l], obuf.at[l], o_s.at[l], o_r.at[l], {"section": l}).wait_recv()
    tokens = jnp.sum(cnts[:, 0:1, 0:1])
    out[...] = obuf[...].astype(F32) / tokens
    for copy in pending:
        copy.wait_send()


def local(
    hidden,
    unembed,
    value_proj,
    output_proj,
    norm_gains,
    survive,
    lengths,
    assign,
    advantage,
    reference_logit,
    recorded_gap,
):
    resp_count, positions, width = hidden.shape
    own, half = value_proj.shape[1:]
    n, ns = lax.axis_size("dp"), lax.axis_size("section")
    rows = resp_count * positions
    sub = own // ns
    q = n * sub
    section = lax.axis_index("section")

    alive = jnp.repeat(survive, GROUP)
    count = jnp.sum((alive * lengths).astype(F32))
    held = jnp.any(assign[None, :] == jnp.arange(resp_count, dtype=assign.dtype)[:, None], axis=1)
    held = jnp.broadcast_to(held[:, None].astype(F32), (resp_count, positions))
    position = lax.broadcasted_iota(jnp.int32, (resp_count, positions), 1)
    live = (position < lengths[:, None]).astype(F32)
    adv = jnp.broadcast_to(advantage[:, None], (resp_count, positions))
    clipped = (adv > 0) & (recorded_gap > clip_high) | (adv < 0) & (recorded_gap < clip_low)
    kept = 1.0 - clipped.astype(F32)
    weight_rows = -loss_scale * adv * kept * live * held
    rowd = jnp.stack(
        [
            weight_rows.reshape(rows),
            reference_logit.reshape(rows),
            held.reshape(rows),
            jnp.broadcast_to(count, (rows,)),
        ]
        * 2
    )
    wown = jnp.concatenate([value_proj[0], output_proj[0].T], axis=1).reshape(ns, sub, 2 * half)
    gown = norm_gains[0].reshape(n, ns, sub).swapaxes(0, 1).reshape(ns, q // 128, 128)
    size = math.lcm(sub, 128)
    lane = jnp.arange(size, dtype=jnp.int32)
    tgt = jnp.broadcast_to((lane // sub * (ns * sub) + section * sub + lane % sub)[None], (8, size))

    dims = (n, ns, rows, sub, half, width)
    steps = n // 2
    vmem = pl.BlockSpec(memory_space=pltpu.VMEM)
    dma = pltpu.SemaphoreType.DMA
    out = pl.pallas_call(
        functools.partial(kernel, dims),
        out_shape=jax.ShapeDtypeStruct((ns, sub, 2 * half), F32),
        in_specs=[vmem] * 6,
        out_specs=vmem,
        scratch_shapes=[
            pltpu.VMEM((ns, n, sub, 2 * half), BF16),
            pltpu.VMEM((ns, q // 128, 128), F32),
            pltpu.VMEM((n, 8, rows), F32),
            pltpu.VMEM((ns, rows, q), BF16),
            pltpu.VMEM((rows, q), BF16),
            pltpu.VMEM((ns, rows, half), BF16),
            pltpu.VMEM((ns, rows, 128), F32),
            pltpu.VMEM((rows, q), BF16),
            pltpu.VMEM((ns, n, sub, 2 * half), BF16),
            pltpu.VMEM((ns, steps, sub, 2 * half), BF16),
            pltpu.VMEM((ns, steps, sub, 2 * half), BF16),
            pltpu.VMEM((ns, sub, 2 * half), BF16),
            pltpu.VMEM((ns, sub, 2 * half), BF16),
            pltpu.VMEM((8, rows, half), BF16),
            pltpu.VMEM((8, ns - 1, rows, half), BF16),
            pltpu.VMEM((ns, 8, rows), F32),
            pltpu.VMEM((ns, ns - 1, 8, rows), F32),
            pltpu.VMEM((6, rows, q), BF16),
            pltpu.VMEM((6, rows, q), BF16),
            pltpu.VMEM((4, 8, rows), F32),
            pltpu.VMEM((4, 8, rows), F32),
            dma((ns - 1,)), dma((ns,)), dma((ns - 1,)), dma((ns,)),
            dma((ns, 2, steps)), dma((ns, 2, steps)), dma((2, steps)), dma((2, steps)),
            dma((8, ns - 1)), dma((8, ns - 1)), dma((ns, ns - 1)), dma((ns, ns - 1)),
            dma((6,)), dma((6,)), dma((4,)), dma((4,)),
            dma((ns, 2, steps)), dma((ns, 2, steps)), dma((ns,)), dma((ns,)),
        ],
        compiler_params=pltpu.CompilerParams(
            collective_id=0, has_side_effects=True, vmem_limit_bytes=60 * 1024 * 1024
        ),
    )(
        hidden.reshape(rows, width),
        unembed.reshape(rows, width),
        wown,
        gown,
        rowd,
        tgt,
    )
    flat = out.reshape(own, 2 * half)
    return (flat[:, :half][None], flat[:, half:].T[None])


def solution(mesh):
    placed = (
        P(("groups", "dp"), None, None),
        P(("groups", "dp"), None, None),
        P("section", "dp", "tensor"),
        P("section", "tensor", "dp"),
        P("section", None),
        P(("groups", "dp")),
        P(("groups", "dp")),
        P(("groups", "dp")),
        P(("groups", "dp")),
        P(("groups", "dp"), None),
        P(("groups", "dp"), None),
    )
    return jax.shard_map(
        local,
        mesh=mesh,
        in_specs=placed,
        out_specs=(
            P(("groups", "section"), "dp", "tensor"),
            P(("groups", "section"), "tensor", "dp"),
        ),
        check_vma=False,
    )
```

time: 456 us -> 207 us (0.45)
  waiting for transfers between devices: 264 us -> 0 us
  Pallas kernels: 0 us -> 192 us
  blocking collectives: 53.1 us -> 0 us
  starting transfers between devices: 32.2 us -> 0 us
  local copies, waits for them, and re-layouts: 34.1 us -> 6.26 us
  other arithmetic: 33 us -> 7.24 us
  matrix products: 20.9 us -> 0 us
  between operations: 15.8 us -> 1.33 us
    pallas_call x0 -> x1, Pallas kernels: none -> 192 us  [local(): pl.pallas_call(functools.partial(kernel, dims), out_shape=jax.ShapeDtypeS...]
    ppermute x8 -> x0, waiting for transfers between devices: 125 us -> none  [from_behind(): return lax.ppermute(block, axis, route)]
    all_gather x1 -> x0, waiting for transfers between devices: 82.2 us -> none  [turned_gather(): result = lax.all_gather(both, axis, axis=0, tiled=True)]
    unnamed x3 -> x0, waiting for transfers between devices: 56.3 us -> none
    all_to_all x8 -> x0, blocking collectives: 53.1 us -> none  [copy_for_each(): lax.all_to_all(jnp.broadcast_to(array[None], (devices, *array.shape)), ax...]
    ppermute x8 -> x0, starting transfers between devices: 23 us -> none  [from_behind(): return lax.ppermute(block, axis, route)]
    dot_general x21 -> x0, matrix products: 20.9 us -> none  [the longest x9 6.51 us: contract_last(): lax.dot_general(left_rows, right_rows, (((1,), (1,)), ((), ())), preferre...]
    unnamed x68 -> x2, local copies, waits for them, and re-layouts: 13.9 us -> 1.27 us
  transfers between devices with their start and end apart: 12 -> 0, of which waited for: 11 -> 0; matrix products, arithmetic and copies ran while one was open for 5% -> 0% of each run, Pallas kernels for 0% -> 0%
where the time goes in v1:
time: 207 us; the launch traced here: 206 us
  Pallas kernels  192 us (93%)
  other arithmetic  7.24 us (3%)
  local copies, waits for them, and re-layouts  6.26 us (3%)
    pallas_call x1, Pallas kernels, local(): pl.pallas_call(functools.partial(kernel, dims), out_shape=jax.ShapeDtypeS...  192 us

profile of v1, /device:TPU:40, one launch (start us, length us, event | category | flops | bytes accessed | tf_op | source)
XLA Modules:
  0.0 206.5 jit_solution(11056362371996152493)
XLA Ops:
  1.3 1.3 convert_reduce_fusion
  2.5 0.6 stack_broadcast_in_dim.4
  3.2 0.8 fusion.4
  4.0 0.7 broadcast_multiply_fusion
  4.6 0.7 broadcast_compare_fusion.1
  5.3 0.7 select_multiply_fusion
  6.0 0.1 copy.22
  6.1 0.1 stack_reshape.12
  6.2 0.1 broadcast_in_dim.17.clone
  6.2 0.1 stack_reshape.14
  6.3 0.8 copy.23
  7.1 0.1 stack_reshape.13
  7.2 0.6 stack.3.rowd
  7.8 0.6 broadcast_in_dim.36.tgt
  8.4 0.5 broadcast.65
  8.9 1.4 reduce.3
  10.3 0.1 reshape_squeeze.3
  10.4 0.7 reshape.53.gown
  11.1 1.7 pad_maximum_fusion.wown
  12.9 191.6 %shard_map.125 = f32[4,80,512]{2,1,0:T(8,128)} custom-call(bf16[128,5120]{1,0:T(8,128)(2,1)} %bitcast.21, bf16[128,5120]{1,0:T(8,128)(2,1)} %bitcast.22, bf16[4,80,512]{2,1,0:T(8,128)(2,1)} %pad_maximum_fusion.wown, f32[4,10,128]{2,1,0:T(8,128)} %reshape.53.gown, f32[8,128]{1,0:T(8,128)} %stack.3.rowd, s32[8,640]{1,0:T(8,128)} %broadcast_in_dim.36.tgt), custom_call_target="tpu_custom_call" | custom-call | tf_op jit(solution)/shard_map/pallas_call | solution.py:395
  204.5 1.9 slice_bitcast_fusion
  (3 shorter events, 0.0 us)

commit v2 on v1

--- a/solution.py
+++ b/solution.py
@@ -8,8 +8,6 @@
 from jax.experimental.pallas import tpu as pltpu
 from jax.sharding import PartitionSpec as P
 
-GROUP = 16
-
 eps_norm = 1e-06
 loss_scale = 4096.0
 clip_high = math.log(1.28)
@@ -34,11 +32,11 @@
 
 def kernel(
     dims,
-    hid, une, wown, gown, rowd, tgt,
+    hid, une, vown, oown, gown, surv, lens, assign, adv, ref_t, gap_t,
     out,
-    wfull, gall, cnts, xs, us, projs, rcols, gcur, wg, rbu, rbd, obuf, osrc,
-    arsrc, arbuf, stsrc, stbuf, dsrc, dbuf, tsrc, tbuf,
-    xa_s, xa_r, ga_s, ga_r, ag_s, ag_r, cn_s, cn_r, ar_s, ar_r, st_s, st_r,
+    xfull, gbuf, wfull, gall, cnts, xs, us, projs, rcols, gcur, wg, rbu, rbd, obuf, osrc,
+    arsrc, arbuf, stsrc, stbuf, dsrc, dbuf, tsrc, tbuf, rowd,
+    l_s, xa_s, xa_r, ga_s, ga_r, ag_s, ag_r, cn_s, cn_r, ar_s, ar_r, st_s, st_r,
     d_s, d_r, t_s, t_r, rs_s, rs_r, o_s, o_r,
 ):
     n, ns, rows, sub, half, width = dims
@@ -65,55 +63,125 @@
     def block(offset):
         return lax.rem(j + n + offset, n)
 
+    part = [pl.ds(0, half), pl.ds(half, half)]
+    owned = [vown, oown]
+    locals_ = [
+        pltpu.make_async_copy(hid, xfull.at[pl.ds(0, rows)], l_s.at[0]),
+        pltpu.make_async_copy(une, xfull.at[pl.ds(rows, rows)], l_s.at[1]),
+        pltpu.make_async_copy(vown.at[s], wfull.at[s, j, :, part[0]], l_s.at[2]),
+        pltpu.make_async_copy(oown.at[s], wfull.at[s, j, :, part[1]], l_s.at[3]),
+    ]
+    for copy in reversed(locals_):
+        copy.start()
+
     barrier = pltpu.get_barrier_semaphore()
     peers = [{"dp": up}, {"dp": down}, {"tensor": other}]
     peers += [{"section": lax.rem(s + k, ns)} for k in range(1, ns)]
     for peer in peers:
         pl.semaphore_signal(barrier, inc=1, device_id=peer, device_id_type=MESH)
+
+    resp, pos = lens.shape[1], ref_t.shape[0]
+    row_index = lax.broadcasted_iota(jnp.int32, (rows, resp), 0)
+    lane_index = lax.broadcasted_iota(jnp.int32, (rows, resp), 1)
+    offset = row_index - lane_index * pos
+    mine = (offset >= 0) & (offset < pos)
+
+    def spread(values):
+        if values.shape[0] == pos:
+            values = jnp.concatenate([values] * resp, axis=0)
+        return jnp.sum(jnp.where(mine, values, 0.0), axis=1, keepdims=True)
+
+    response = spread(lane_index.astype(F32))
+    held = jnp.max(
+        jnp.where(assign[...].astype(F32) == response, 1.0, 0.0), axis=1, keepdims=True
+    )
+    live = jnp.sum(jnp.where(mine & (offset < lens[...]), 1.0, 0.0), axis=1, keepdims=True)
+    adv_col = spread(adv[...])
+    gap_col = spread(gap_t[...])
+    clipped = (adv_col > 0) & (gap_col > clip_high) | (adv_col < 0) & (gap_col < clip_low)
+    rowd[0] = jnp.broadcast_to(
+        jnp.where(clipped, 0.0, -loss_scale * adv_col * live * held), (rows, 128)
+    )
+    rowd[1] = jnp.broadcast_to(spread(ref_t[...]), (rows, 128))
+    rowd[2] = jnp.broadcast_to(held, (rows, 128))
+    gbuf[s] = gown[...]
+    tokens_here = jnp.sum((surv[...] * lens[...]).astype(F32), axis=1, keepdims=True)
+    cnts[j] = jnp.broadcast_to(tokens_here, cnts.shape[1:])
+
     pl.semaphore_wait(barrier, len(peers))
+
+    def hand_out():
+        for k in range(1, ns):
+            to = lax.rem(s + k, ns)
+            for p in range(2):
+                remote(
+                    owned[p].at[to], wfull.at[s, j, :, part[p]],
+                    xa_s.at[p, k - 1], xa_r.at[p, s], {"section": to},
+                ).start()
 
     for k in range(1, ns):
         to = lax.rem(s + k, ns)
-        go(wown.at[to], wfull.at[s, j], xa_s.at[k - 1], xa_r.at[s], {"section": to})
-        go(gown.at[to], gall.at[s], ga_s.at[k - 1], ga_r.at[s], {"section": to})
-    wfull[s, j] = wown[s]
-    gall[s] = gown[s]
-    cnts[j] = jnp.broadcast_to(rowd[3:4, :], cnts.shape[1:])
+        go(gown, gbuf.at[s], ga_s.at[k - 1], ga_r.at[s], {"section": to})
+        for p in range(2):
+            pending.append(
+                remote(
+                    owned[p].at[to], wfull.at[s, j, :, part[p]],
+                    xa_s.at[p, k - 1], xa_r.at[p, s], {"section": to},
+                )
+            )
+    pl.when(s < 2)(hand_out)
+    for copy in locals_[2:]:
+        copy.wait()
 
     def layer_arrived(l):
         @pl.when(s != l)
         def _():
             away = {"section": lax.rem(s + 1, ns)}
-            remote(wown.at[0], wfull.at[l, j], xa_s.at[0], xa_r.at[l], away).wait_recv()
-            remote(gown.at[0], gall.at[l], ga_s.at[0], ga_r.at[l], away).wait_recv()
+            for p in range(2):
+                remote(owned[p].at[0], wfull.at[l, j, :, part[p]], xa_s.at[p, 0], xa_r.at[p, l], away).wait_recv()
 
     steps = n // 2
 
-    def reach(l, way):
-        return steps if (l + way) % 2 == 0 else steps - 1
+    def reach(l, p, way):
+        return steps if (l + p + way) % 2 == 0 else steps - 1
 
     toward = [{"dp": up}, {"dp": down}]
     sign = [1, -1]
 
-    def ag_send(l, k, way):
-        if k <= reach(l, way):
+    def ag_copy(l, p, k, way, b):
+        piece = wfull.at[l, b, :, part[p]]
+        at = (l, p, way, k - 1)
+        return (piece, piece, ag_s.at[at], ag_r.at[at], toward[way])
+
+    def cn_copy(k, way, b):
+        return (cnts.at[b], cnts.at[b], cn_s.at[way, k - 1], cn_r.at[way, k - 1], toward[way])
+
+    def ag_send(l, p, k, way):
+        if k <= reach(l, p, way):
             b = block(-sign[way] * (k - 1))
-            go(wfull.at[l, b], wfull.at[l, b], ag_s.at[l, way, k - 1], ag_r.at[l, way, k - 1], toward[way])
-            if l == 0:
-                go(cnts.at[b], cnts.at[b], cn_s.at[way, k - 1], cn_r.at[way, k - 1], toward[way])
-
-    def ag_recv(l, k, way):
-        if k <= reach(l, way):
+            go(*ag_copy(l, p, k, way, b))
+            if l == 0 and p == 0:
+                go(*cn_copy(k, way, b))
+
+    def ag_recv(l, p, k, way):
+        if k <= reach(l, p, way):
             b = block(-sign[way] * k)
-            remote(wfull.at[l, b], wfull.at[l, b], ag_s.at[l, way, k - 1], ag_r.at[l, way, k - 1], toward[way]).wait_recv()
-            if l == 0:
-                remote(cnts.at[b], cnts.at[b], cn_s.at[way, k - 1], cn_r.at[way, k - 1], toward[way]).wait_recv()
+            remote(*ag_copy(l, p, k, way, b)).wait_recv()
+            if l == 0 and p == 0:
+                remote(*cn_copy(k, way, b)).wait_recv()
 
     def ag_tick(ls, k):
         for l in ls:
+            for p in range(2):
+                for way in range(2):
+                    ag_recv(l, p, k, way)
+                    ag_send(l, p, k + 1, way)
+
+    def ag_start(l):
+        layer_arrived(l)
+        for p in range(2):
             for way in range(2):
-                ag_recv(l, k, way)
-                ag_send(l, k + 1, way)
+                ag_send(l, p, 1, way)
 
     eye = lax.broadcasted_iota(jnp.int32, (rows, rows), 0) == lax.broadcasted_iota(jnp.int32, (rows, rows), 1)
 
@@ -128,7 +196,7 @@
         return w.reshape(q, half)
 
     def gain(l):
-        return jnp.concatenate([gall[l, i : i + 1, :] for i in range(q // 128)], axis=1)
+        return gall[l : l + 1, :]
 
     def ar_send(i, value, stats=None):
         arsrc[i] = value
@@ -173,19 +241,38 @@
         return to_col(tsrc[i, 0:1, :] + tbuf[i, 0:1, :])
 
     def select_features():
-        size = tgt.shape[1]
+        for l in range(layers):
+            @pl.when(s != l)
+            def _():
+                away = {"section": lax.rem(s + 1, ns)}
+                remote(gown, gbuf.at[l], ga_s.at[0], ga_r.at[l], away).wait_recv()
+        gains = gbuf[:, 0, :]
+        high = gains.astype(BF16).astype(F32)
+        middle = (gains - high).astype(BF16).astype(F32)
+        low = gains - high - middle
+        pad = jnp.zeros((16 - 3 * layers, width), F32)
+        xfull[2 * rows :, :] = jnp.concatenate([high, middle, low, pad], axis=0).astype(BF16)
+        for copy in locals_[:2]:
+            copy.wait()
+        size = math.lcm(sub, 128)
         place = lax.broadcasted_iota(jnp.int32, (size, size), 0)
-        for super_index in range(width // (4 * size)):
+        lane = lax.broadcasted_iota(jnp.int32, (size, size), 1)
+        slices = jnp.zeros((size, size), jnp.int32)
+        for m in range(1, size // sub):
+            slices = slices + (lane >= m * sub).astype(jnp.int32)
+        target = lane + slices * ((ns - 1) * sub) + s * sub
+        for super_index in range(width // (ns * size)):
             total = None
             for c in range(ns):
-                pick = (place + c * size == tgt[0:1, :]).astype(F32).astype(BF16)
+                pick = (place + c * size == target).astype(F32).astype(BF16)
                 at = (super_index * ns + c) * size
-                lhs = jnp.concatenate([hid[:, at : at + size], une[:, at : at + size]], axis=0)
-                piece = dot_nn(lhs, pick)
+                piece = dot_nn(xfull[:, at : at + size], pick)
                 total = piece if total is None else total + piece
-            total = total.astype(BF16)
-            xs[0, :, super_index * size : (super_index + 1) * size] = total[:rows]
-            us[:, super_index * size : (super_index + 1) * size] = total[rows:]
+            span = slice(super_index * size, (super_index + 1) * size)
+            xs[0, :, span] = total[:rows].astype(BF16)
+            us[:, span] = total[rows : 2 * rows].astype(BF16)
+            parts = total[2 * rows : 2 * rows + 16]
+            gall[:, span] = parts[:layers] + parts[layers : 2 * layers] + parts[2 * layers : 3 * layers]
 
     def contribute(l):
         x = xs[l].astype(F32)
@@ -226,17 +313,14 @@
         yield
 
     for l in (0, 1):
-        layer_arrived(l)
-        for way in range(2):
-            ag_send(l, 1, way)
+        ag_start(l)
+    pl.when(s >= 2)(hand_out)
     select_features()
     for k in range(1, steps + 1):
         ag_tick((0, 1), k)
         if k == steps:
             for l in (2, 3):
-                layer_arrived(l)
-                for way in range(2):
-                    ag_send(l, 1, way)
+                ag_start(l)
     stage = early()
     for k in range(1, steps + 1):
         next(stage, None)
@@ -261,24 +345,34 @@
 
     landing = [rbu, rbd]
 
-    def rs_send(l, i, way):
-        hops = reach(l, way)
+    def rs_copy(l, p, i, way, b):
+        at = (l, p, way, i - 1)
+        return (
+            wg.at[l, b, :, part[p]], landing[way].at[l, i - 1, :, part[p]],
+            rs_s.at[at], rs_r.at[at], toward[way],
+        )
+
+    def rs_send(l, p, i, way):
+        hops = reach(l, p, way)
         if i <= hops:
-            b = block(sign[way] * (hops - i + 1))
-            go(wg.at[l, b], landing[way].at[l, i - 1], rs_s.at[l, way, i - 1], rs_r.at[l, way, i - 1], toward[way])
-
-    def rs_recv(l, i, way):
-        hops = reach(l, way)
+            go(*rs_copy(l, p, i, way, block(sign[way] * (hops - i + 1))))
+
+    def rs_recv(l, p, i, way):
+        hops = reach(l, p, way)
         if i <= hops:
             b = block(sign[way] * (hops - i))
-            remote(wg.at[l, b], landing[way].at[l, i - 1], rs_s.at[l, way, i - 1], rs_r.at[l, way, i - 1], toward[way]).wait_recv()
-            wg[l, b] = (wg[l, b].astype(F32) + landing[way][l, i - 1].astype(F32)).astype(BF16)
+            remote(*rs_copy(l, p, i, way, b)).wait_recv()
+            cols = slice(p * half, (p + 1) * half)
+            wg[l, b, :, cols] = (
+                wg[l, b, :, cols].astype(F32) + landing[way][l, i - 1, :, cols].astype(F32)
+            ).astype(BF16)
 
     position = {}
 
     def rs_start(l):
-        for way in range(2):
-            rs_send(l, 1, way)
+        for p in range(2):
+            for way in range(2):
+                rs_send(l, p, 1, way)
         position[l] = 1
 
     def rs_tick():
@@ -286,9 +380,10 @@
             i = position[l]
             if i > steps:
                 continue
-            for way in range(2):
-                rs_recv(l, i, way)
-                rs_send(l, i + 1, way)
+            for p in range(2):
+                for way in range(2):
+                    rs_recv(l, p, i, way)
+                    rs_send(l, p, i + 1, way)
             position[l] = i + 1
             if i == steps:
                 finish(l)
@@ -304,9 +399,7 @@
         def _():
             remote(osrc.at[l], obuf.at[s], o_s.at[l], o_r.at[s], {"section": l}).start()
 
-    wcol = to_col(rowd[0:1, :])
-    base = to_col(rowd[1:2, :])
-    held = to_col(rowd[2:3, :])
+    wcol, base, held = rowd[0, :, 0:1], rowd[1, :, 0:1], rowd[2, :, 0:1]
     inner = to_col(inner_row)
     logit = inner + small_recv(3)
     seed = wcol * jnp.exp(jnp.where(held > 0.0, logit - base, 0.0))
@@ -317,6 +410,8 @@
         small_send(l - 1, jnp.sum(gp.astype(F32) * projs[l].astype(F32), axis=1, keepdims=True))
         wgrad(l, gp)
         rs_start(l)
+        if l < layers - 1:
+            rs_tick()
         grad_normed = pair_recv(2 + l)
         inverse = rcols[l, :, 0:1]
         inner = small_recv(l - 1) * (inverse * inverse) / width
@@ -324,6 +419,7 @@
             gcur[...].astype(F32) + inverse * gain(l) * grad_normed - xs[l].astype(F32) * inner
         ).astype(BF16)
         ar_send(4 + l, dot_nn(gcur[...], weight(l - 1, False)).astype(BF16))
+        rs_tick()
         rs_tick()
         gp = ar_recv(4 + l).astype(BF16)
     wgrad(0, gp)
@@ -361,45 +457,21 @@
     rows = resp_count * positions
     sub = own // ns
     q = n * sub
-    section = lax.axis_index("section")
-
-    alive = jnp.repeat(survive, GROUP)
-    count = jnp.sum((alive * lengths).astype(F32))
-    held = jnp.any(assign[None, :] == jnp.arange(resp_count, dtype=assign.dtype)[:, None], axis=1)
-    held = jnp.broadcast_to(held[:, None].astype(F32), (resp_count, positions))
-    position = lax.broadcasted_iota(jnp.int32, (resp_count, positions), 1)
-    live = (position < lengths[:, None]).astype(F32)
-    adv = jnp.broadcast_to(advantage[:, None], (resp_count, positions))
-    clipped = (adv > 0) & (recorded_gap > clip_high) | (adv < 0) & (recorded_gap < clip_low)
-    kept = 1.0 - clipped.astype(F32)
-    weight_rows = -loss_scale * adv * kept * live * held
-    rowd = jnp.stack(
-        [
-            weight_rows.reshape(rows),
-            reference_logit.reshape(rows),
-            held.reshape(rows),
-            jnp.broadcast_to(count, (rows,)),
-        ]
-        * 2
-    )
-    wown = jnp.concatenate([value_proj[0], output_proj[0].T], axis=1).reshape(ns, sub, 2 * half)
-    gown = norm_gains[0].reshape(n, ns, sub).swapaxes(0, 1).reshape(ns, q // 128, 128)
-    size = math.lcm(sub, 128)
-    lane = jnp.arange(size, dtype=jnp.int32)
-    tgt = jnp.broadcast_to((lane // sub * (ns * sub) + section * sub + lane % sub)[None], (8, size))
-
     dims = (n, ns, rows, sub, half, width)
     steps = n // 2
     vmem = pl.BlockSpec(memory_space=pltpu.VMEM)
+    anywhere = pl.BlockSpec(memory_space=pl.ANY)
     dma = pltpu.SemaphoreType.DMA
     out = pl.pallas_call(
         functools.partial(kernel, dims),
         out_shape=jax.ShapeDtypeStruct((ns, sub, 2 * half), F32),
-        in_specs=[vmem] * 6,
+        in_specs=[anywhere] * 4 + [vmem] * 7,
         out_specs=vmem,
         scratch_shapes=[
+            pltpu.VMEM((2 * rows + 16, width), BF16),
+            pltpu.VMEM((ns, 1, width), F32),
             pltpu.VMEM((ns, n, sub, 2 * half), BF16),
-            pltpu.VMEM((ns, q // 128, 128), F32),
+            pltpu.VMEM((ns, q), F32),
             pltpu.VMEM((n, 8, rows), F32),
             pltpu.VMEM((ns, rows, q), BF16),
             pltpu.VMEM((rows, q), BF16),
@@ -419,11 +491,12 @@
             pltpu.VMEM((6, rows, q), BF16),
             pltpu.VMEM((4, 8, rows), F32),
             pltpu.VMEM((4, 8, rows), F32),
-            dma((ns - 1,)), dma((ns,)), dma((ns - 1,)), dma((ns,)),
-            dma((ns, 2, steps)), dma((ns, 2, steps)), dma((2, steps)), dma((2, steps)),
+            pltpu.VMEM((3, rows, 128), F32),
+            dma((4,)), dma((2, ns - 1)), dma((2, ns)), dma((ns - 1,)), dma((ns,)),
+            dma((ns, 2, 2, steps)), dma((ns, 2, 2, steps)), dma((2, steps)), dma((2, steps)),
             dma((8, ns - 1)), dma((8, ns - 1)), dma((ns, ns - 1)), dma((ns, ns - 1)),
             dma((6,)), dma((6,)), dma((4,)), dma((4,)),
-            dma((ns, 2, steps)), dma((ns, 2, steps)), dma((ns,)), dma((ns,)),
+            dma((ns, 2, 2, steps)), dma((ns, 2, 2, steps)), dma((ns,)), dma((ns,)),
         ],
         compiler_params=pltpu.CompilerParams(
             collective_id=0, has_side_effects=True, vmem_limit_bytes=60 * 1024 * 1024
@@ -431,10 +504,15 @@
     )(
         hidden.reshape(rows, width),
         unembed.reshape(rows, width),
-        wown,
-        gown,
-        rowd,
-        tgt,
+        value_proj.reshape(ns, sub, half),
+        output_proj[0].T.reshape(ns, sub, half),
+        norm_gains,
+        survive.reshape(1, 1),
+        lengths.reshape(1, resp_count),
+        assign.reshape(1, resp_count),
+        advantage.reshape(1, resp_count),
+        reference_logit.T,
+        recorded_gap.T,
     )
     flat = out.reshape(own, 2 * half)
     return (flat[:, :half][None], flat[:, half:].T[None])

time: 207 us -> 191 us (0.923)
  other arithmetic: 7.24 us -> 0 us
  Pallas kernels: 192 us -> 187 us
  local copies, waits for them, and re-layouts: 6.26 us -> 1.95 us
    pallas_call x1, Pallas kernels: 192 us -> 187 us  [local(): pl.pallas_call(functools.partial(kernel, dims), out_shape=jax.ShapeDtypeS...]
where the time goes in v2:
time: 191 us; the launch traced here: 190 us
  Pallas kernels  187 us (98%)
  local copies, waits for them, and re-layouts  1.95 us (1%)
    pallas_call x1, Pallas kernels, local(): pl.pallas_call(functools.partial(kernel, dims), out_shape=jax.ShapeDtypeS...  187 us

profile of v2, /device:TPU:40, one launch (start us, length us, event | category | flops | bytes accessed | tf_op | source)
XLA Modules:
  0.0 190.5 jit_solution(11836829780507553308)
XLA Ops:
  1.3 187.3 %shard_map.122 = f32[4,80,512]{2,1,0:T(8,128)} custom-call(bf16[128,5120]{1,0:T(8,128)(2,1)} %bitcast.23, bf16[128,5120]{1,0:T(8,128)(2,1)} %bitcast.24, bf16[4,80,256]{2,1,0:T(8,128)(2,1)} %bitcast.25, bf16[4,80,256]{2,1,0:T(8,128)(2,1)} %bitcast.26, f32[1,5120]{1,0:T(1,128)} %gown.1, s32[1,1]{1,0:T(1,128)} %bitcast.21.surv, s32[1,16]{1,0:T(1,128)} %bitcast.29, ...), custom_call_target="tpu_custom_call" | custom-call | tf_op jit(solution)/shard_map/pallas_call | solution.py:465
  188.5 1.9 %slice_bitcast_fusion = (f32[1,256,320]{1,2,0:T(8,128)}, f32[1,320,256]{2,1,0:T(8,128)}) fusion(f32[320,512]{1,0:T(8,128)} %bitcast.22), kind=kLoop, calls=%fused_computation | loop fusion | bytes 1310720 | tf_op jit(solution)/shard_map/broadcast_in_dim | solution.py:518

commit v3 on v2

--- a/solution.py
+++ b/solution.py
@@ -17,6 +17,10 @@
 BF16 = jnp.bfloat16
 MESH = pl.DeviceIdType.MESH
 
+RING_START = (0, 0, 5, 8)
+CHAIN_AT = (8, 10, 13, 16)
+RING_STEPS = ((0, 1), (0, 1), (0, 1))
+
 
 def dot_nn(a, b):
     return jnp.dot(a, b, preferred_element_type=F32)
@@ -34,14 +38,15 @@
     dims,
     hid, une, vown, oown, gown, surv, lens, assign, adv, ref_t, gap_t,
     out,
-    xfull, gbuf, wfull, gall, cnts, xs, us, projs, rcols, gcur, wg, rbu, rbd, obuf, osrc,
-    arsrc, arbuf, stsrc, stbuf, dsrc, dbuf, tsrc, tbuf, rowd,
+    xfull, gbuf, wfull, wpeer, gall, cnts, xs, us, projs, rcols, wg, rbu, rbd, obuf, osrc,
+    arsrc, arbuf, stsrc, stbuf, nrows, grows, prows, qrows, psrc, qsrc, rowd, picks,
     l_s, xa_s, xa_r, ga_s, ga_r, ag_s, ag_r, cn_s, cn_r, ar_s, ar_r, st_s, st_r,
-    d_s, d_r, t_s, t_r, rs_s, rs_r, o_s, o_r,
+    pw_s, pw_r, ex_s, ex_r, rs_s, rs_r, o_s, o_r,
 ):
     n, ns, rows, sub, half, width = dims
     q = n * sub
     layers = ns
+    mine_rows = rows // 2
     j = lax.axis_index("dp")
     s = lax.axis_index("section")
     t = lax.axis_index("tensor")
@@ -66,8 +71,8 @@
     part = [pl.ds(0, half), pl.ds(half, half)]
     owned = [vown, oown]
     locals_ = [
-        pltpu.make_async_copy(hid, xfull.at[pl.ds(0, rows)], l_s.at[0]),
-        pltpu.make_async_copy(une, xfull.at[pl.ds(rows, rows)], l_s.at[1]),
+        pltpu.make_async_copy(hid.at[t], xfull.at[pl.ds(0, mine_rows)], l_s.at[0]),
+        pltpu.make_async_copy(une.at[t], xfull.at[pl.ds(mine_rows, mine_rows)], l_s.at[1]),
         pltpu.make_async_copy(vown.at[s], wfull.at[s, j, :, part[0]], l_s.at[2]),
         pltpu.make_async_copy(oown.at[s], wfull.at[s, j, :, part[1]], l_s.at[3]),
     ]
@@ -81,14 +86,14 @@
         pl.semaphore_signal(barrier, inc=1, device_id=peer, device_id_type=MESH)
 
     resp, pos = lens.shape[1], ref_t.shape[0]
-    row_index = lax.broadcasted_iota(jnp.int32, (rows, resp), 0)
-    lane_index = lax.broadcasted_iota(jnp.int32, (rows, resp), 1)
+    row_index = lax.broadcasted_iota(jnp.int32, (mine_rows, resp), 0) + t * mine_rows
+    lane_index = lax.broadcasted_iota(jnp.int32, (mine_rows, resp), 1)
     offset = row_index - lane_index * pos
     mine = (offset >= 0) & (offset < pos)
 
     def spread(values):
         if values.shape[0] == pos:
-            values = jnp.concatenate([values] * resp, axis=0)
+            values = jnp.concatenate([values] * (mine_rows // pos), axis=0)
         return jnp.sum(jnp.where(mine, values, 0.0), axis=1, keepdims=True)
 
     response = spread(lane_index.astype(F32))
@@ -100,10 +105,10 @@
     gap_col = spread(gap_t[...])
     clipped = (adv_col > 0) & (gap_col > clip_high) | (adv_col < 0) & (gap_col < clip_low)
     rowd[0] = jnp.broadcast_to(
-        jnp.where(clipped, 0.0, -loss_scale * adv_col * live * held), (rows, 128)
+        jnp.where(clipped, 0.0, -loss_scale * adv_col * live * held), (mine_rows, 128)
     )
-    rowd[1] = jnp.broadcast_to(spread(ref_t[...]), (rows, 128))
-    rowd[2] = jnp.broadcast_to(held, (rows, 128))
+    rowd[1] = jnp.broadcast_to(spread(ref_t[...]), (mine_rows, 128))
+    rowd[2] = jnp.broadcast_to(held, (mine_rows, 128))
     gbuf[s] = gown[...]
     tokens_here = jnp.sum((surv[...] * lens[...]).astype(F32), axis=1, keepdims=True)
     cnts[j] = jnp.broadcast_to(tokens_here, cnts.shape[1:])
@@ -170,20 +175,34 @@
             if l == 0 and p == 0:
                 remote(*cn_copy(k, way, b)).wait_recv()
 
-    def ag_tick(ls, k):
-        for l in ls:
-            for p in range(2):
-                for way in range(2):
-                    ag_recv(l, p, k, way)
-                    ag_send(l, p, k + 1, way)
+    def peer_copy(l, slot, b):
+        return (wfull.at[l, b], wpeer.at[l, b], pw_s.at[l, slot], pw_r.at[l, slot], {"tensor": other})
+
+    def peer_arrived(l):
+        remote(*peer_copy(l, 0, j)).wait_recv()
+        for slot in range(1, n):
+            remote(*peer_copy(l, slot, j)).wait_recv()
+
+    def ag_tick(tick):
+        for l in range(layers):
+            k = tick - RING_START[l]
+            if 1 <= k <= steps:
+                for p in range(2):
+                    for way in range(2):
+                        ag_recv(l, p, k, way)
+                        ag_send(l, p, k + 1, way)
+                go(*peer_copy(l, 2 * k - 1, block(-k)))
+                if k < steps:
+                    go(*peer_copy(l, 2 * k, block(k)))
 
     def ag_start(l):
         layer_arrived(l)
         for p in range(2):
             for way in range(2):
                 ag_send(l, p, 1, way)
-
-    eye = lax.broadcasted_iota(jnp.int32, (rows, rows), 0) == lax.broadcasted_iota(jnp.int32, (rows, rows), 1)
+        go(*peer_copy(l, 0, j))
+
+    eye = lax.broadcasted_iota(jnp.int32, (mine_rows, 128), 0) == lax.broadcasted_iota(jnp.int32, (mine_rows, 128), 1)
 
     def to_row(column):
         return jnp.sum(jnp.where(eye, column, 0.0), axis=0, keepdims=True)
@@ -191,9 +210,17 @@
     def to_col(row):
         return jnp.sum(jnp.where(eye, row, 0.0), axis=1, keepdims=True)
 
-    def weight(l, first):
-        w = wfull[l, :, :, 0:half] if first else wfull[l, :, :, half : 2 * half]
-        return w.reshape(q, half)
+    def forward_dot(rows_in, l, which):
+        cols = slice(which * half, (which + 1) * half)
+        return jnp.concatenate(
+            [dot_nn(rows_in, w[l, :, :, cols].reshape(q, half)) for w in (wfull, wpeer)], axis=1
+        )
+
+    def backward_dot(rows_in, l, which):
+        cols = slice(which * half, (which + 1) * half)
+        return dot_nt(rows_in[:, :half], wfull[l, :, :, cols].reshape(q, half)) + dot_nt(
+            rows_in[:, half:], wpeer[l, :, :, cols].reshape(q, half)
+        )
 
     def gain(l):
         return gall[l : l + 1, :]
@@ -201,7 +228,7 @@
     def ar_send(i, value, stats=None):
         arsrc[i] = value
         if stats is not None:
-            first = lax.broadcasted_iota(jnp.int32, (8, rows), 0) == 0
+            first = lax.broadcasted_iota(jnp.int32, (8, 128), 0) == 0
             stsrc[i] = jnp.where(first, stats[0], stats[1])
         for k in range(1, ns):
             to = {"section": lax.rem(s + k, ns)}
@@ -224,23 +251,35 @@
             total = total + arbuf[i, k - 1].astype(F32)
         return (total, both) if stats else total
 
-    def pair_send(i, value):
-        dsrc[i] = value
-        go(dsrc.at[i], dbuf.at[i], d_s.at[i], d_r.at[i], {"tensor": other})
-
-    def pair_recv(i):
-        remote(dsrc.at[i], dbuf.at[i], d_s.at[i], d_r.at[i], {"tensor": other}).wait_recv()
-        return dsrc[i].astype(F32) + dbuf[i].astype(F32)
-
-    def small_send(i, column):
-        tsrc[i] = jnp.broadcast_to(to_row(column), (8, rows))
-        go(tsrc.at[i], tbuf.at[i], t_s.at[i], t_r.at[i], {"tensor": other})
-
-    def small_recv(i):
-        remote(tsrc.at[i], tbuf.at[i], t_s.at[i], t_r.at[i], {"tensor": other}).wait_recv()
-        return to_col(tsrc[i, 0:1, :] + tbuf[i, 0:1, :])
+    def swap_copy(kind, l):
+        held_rows = (nrows, grows)[kind] if kind < 2 else (prows, qrows)[kind - 2]
+        source = held_rows.at[l, pl.ds(0, mine_rows)] if kind < 2 else (psrc, qsrc)[kind - 2].at[l]
+        return (
+            source, held_rows.at[l, pl.ds(mine_rows, mine_rows)],
+            ex_s.at[kind, l], ex_r.at[kind, l], {"tensor": other},
+        )
+
+    def swap(kind, l, value):
+        if kind < 2:
+            (nrows, grows)[kind][l, 0:mine_rows] = value
+        else:
+            (prows, qrows)[kind - 2][l, 0:mine_rows] = value[:, :half]
+            (psrc, qsrc)[kind - 2][l] = value[:, half:]
+        go(*swap_copy(kind, l))
+
+    def swapped(kind, l):
+        remote(*swap_copy(kind, l)).wait_recv()
 
     def select_features():
+        size = math.lcm(sub, 128)
+        place = lax.broadcasted_iota(jnp.int32, (size, size), 0)
+        lane = lax.broadcasted_iota(jnp.int32, (size, size), 1)
+        slices = jnp.zeros((size, size), jnp.int32)
+        for m in range(1, size // sub):
+            slices = slices + (lane >= m * sub).astype(jnp.int32)
+        target = lane + slices * ((ns - 1) * sub) + s * sub - place
+        for c in range(ns):
+            picks[c] = (target == c * size).astype(F32).astype(BF16)
         for l in range(layers):
             @pl.when(s != l)
             def _():
@@ -251,33 +290,26 @@
         middle = (gains - high).astype(BF16).astype(F32)
         low = gains - high - middle
         pad = jnp.zeros((16 - 3 * layers, width), F32)
-        xfull[2 * rows :, :] = jnp.concatenate([high, middle, low, pad], axis=0).astype(BF16)
+        xfull[2 * mine_rows :, :] = jnp.concatenate([high, middle, low, pad], axis=0).astype(BF16)
         for copy in locals_[:2]:
             copy.wait()
-        size = math.lcm(sub, 128)
-        place = lax.broadcasted_iota(jnp.int32, (size, size), 0)
-        lane = lax.broadcasted_iota(jnp.int32, (size, size), 1)
-        slices = jnp.zeros((size, size), jnp.int32)
-        for m in range(1, size // sub):
-            slices = slices + (lane >= m * sub).astype(jnp.int32)
-        target = lane + slices * ((ns - 1) * sub) + s * sub
         for super_index in range(width // (ns * size)):
             total = None
             for c in range(ns):
-                pick = (place + c * size == target).astype(F32).astype(BF16)
                 at = (super_index * ns + c) * size
-                piece = dot_nn(xfull[:, at : at + size], pick)
+                piece = dot_nn(xfull[:, at : at + size], picks[c])
                 total = piece if total is None else total + piece
             span = slice(super_index * size, (super_index + 1) * size)
-            xs[0, :, span] = total[:rows].astype(BF16)
-            us[:, span] = total[rows : 2 * rows].astype(BF16)
-            parts = total[2 * rows : 2 * rows + 16]
+            xs[0, :, span] = total[:mine_rows].astype(BF16)
+            us[:, span] = total[mine_rows : 2 * mine_rows].astype(BF16)
+            parts = total[2 * mine_rows : 2 * mine_rows + 16]
             gall[:, span] = parts[:layers] + parts[layers : 2 * layers] + parts[2 * layers : 3 * layers]
 
     def contribute(l):
+        peer_arrived(l)
         x = xs[l].astype(F32)
         xg = (x * gain(l)).astype(BF16)
-        partial = dot_nn(xg, weight(l, True)).astype(BF16)
+        partial = forward_dot(xg, l, 0).astype(BF16)
         squares = to_row(jnp.sum(x * x, axis=1, keepdims=True))
         inner = squares
         if l == layers - 1:
@@ -287,61 +319,64 @@
     def collect(l):
         total, both = ar_recv(l, True)
         inverse = lax.rsqrt(to_col(both[0:1, :]) / width + eps_norm)
-        rcols[l] = jnp.broadcast_to(inverse, (rows, 128))
-        projs[l] = (total * inverse).astype(BF16)
+        rcols[l] = jnp.broadcast_to(inverse, (mine_rows, 128))
+        proj = (total * inverse).astype(BF16)
+        projs[l] = proj
+        if l < layers - 1:
+            mixed = backward_dot(proj, l, 1)
+            xs[l + 1] = (xs[l].astype(F32) + mixed).astype(BF16)
         return both[1:2, :]
 
-    def mix(l):
-        pair_send(l, dot_nt(projs[l], weight(l, False)).astype(BF16))
-
-    def advance(l):
-        xs[l + 1] = (xs[l].astype(F32) + pair_recv(l)).astype(BF16)
-
-    def early():
+    def share(l):
+        swap(0, l, (xs[l].astype(F32) * rcols[l, :, 0:1] * gain(l)).astype(BF16))
+        swap(2, l, projs[l])
+
+    def chain():
         contribute(0)
         yield
         collect(0)
-        mix(0)
-        yield
-        advance(0)
         contribute(1)
+        share(0)
         yield
         collect(1)
-        mix(1)
+        contribute(2)
+        share(1)
         yield
-        advance(1)
+        collect(2)
+        contribute(3)
+        ar_send(4, forward_dot(us[...], 3, 1).astype(BF16))
+        share(2)
         yield
 
-    for l in (0, 1):
-        ag_start(l)
-    pl.when(s >= 2)(hand_out)
-    select_features()
-    for k in range(1, steps + 1):
-        ag_tick((0, 1), k)
-        if k == steps:
-            for l in (2, 3):
+    stage = chain()
+    for tick in range(max(RING_START) + steps + 1):
+        if tick > 0:
+            ag_tick(tick)
+        for l in range(layers):
+            if tick == RING_START[l]:
                 ag_start(l)
-    stage = early()
-    for k in range(1, steps + 1):
-        next(stage, None)
-        ag_tick((2, 3), k)
+        if tick == 0:
+            pl.when(s >= 2)(hand_out)
+            select_features()
+        for _ in range(CHAIN_AT.count(tick)):
+            next(stage)
     for _ in stage:
         pass
-
-    contribute(2)
-    ar_send(4, dot_nn(us[...], weight(3, False)).astype(BF16))
-    collect(2)
-    mix(2)
-    advance(2)
-    contribute(3)
     inner_row = collect(3)
     top = ar_recv(4)
-    small_send(3, jnp.sum(projs[3].astype(F32) * top, axis=1, keepdims=True))
-
-    def wgrad(l, gp):
-        normed = (xs[l].astype(F32) * rcols[l, :, 0:1] * gain(l)).astype(BF16)
-        wg[l, :, :, 0:half] = dot_tn(normed, gp).astype(BF16).reshape(n, sub, half)
-        wg[l, :, :, half : 2 * half] = dot_tn(gcur[...], projs[l]).astype(BF16).reshape(n, sub, half)
+    share(3)
+
+    def wgrad_value(l):
+        swapped(0, l)
+        swapped(3, l)
+        wg[l, :, :, 0:half] = dot_tn(nrows[l], qrows[l]).astype(BF16).reshape(n, sub, half)
+        rs_start(l, 0)
+
+    def wgrad_output(l):
+        swapped(1, l)
+        swapped(2, l)
+        wg[l, :, :, half : 2 * half] = dot_tn(grows[l], prows[l]).astype(BF16).reshape(n, sub, half)
+        rs_start(l, 1)
 
     landing = [rbu, rbd]
 
@@ -369,24 +404,26 @@
 
     position = {}
 
-    def rs_start(l):
-        for p in range(2):
-            for way in range(2):
-                rs_send(l, p, 1, way)
-        position[l] = 1
+    def rs_start(l, p):
+        for way in range(2):
+            rs_send(l, p, 1, way)
+        position[l, p] = 1
 
     def rs_tick():
-        for l in sorted(position, reverse=True):
-            i = position[l]
+        for l, p in sorted(position, reverse=True):
+            i = position[l, p]
             if i > steps:
                 continue
-            for p in range(2):
-                for way in range(2):
-                    rs_recv(l, p, i, way)
-                    rs_send(l, p, i + 1, way)
-            position[l] = i + 1
-            if i == steps:
+            for way in range(2):
+                rs_recv(l, p, i, way)
+                rs_send(l, p, i + 1, way)
+            position[l, p] = i + 1
+            if i == steps and position.get((l, 1 - p), 0) > steps:
                 finish(l)
+
+    def rs_ticks(count):
+        for _ in range(count):
+            rs_tick()
 
     def finish(l):
         osrc[l] = wg[l, j]
@@ -401,29 +438,33 @@
 
     wcol, base, held = rowd[0, :, 0:1], rowd[1, :, 0:1], rowd[2, :, 0:1]
     inner = to_col(inner_row)
-    logit = inner + small_recv(3)
+    logit = inner + jnp.sum(projs[3].astype(F32) * top, axis=1, keepdims=True)
     seed = wcol * jnp.exp(jnp.where(held > 0.0, logit - base, 0.0))
+    upstream = (seed * us[...].astype(F32)).astype(BF16)
     gp = (seed * top).astype(BF16)
-    gcur[...] = (seed * us[...].astype(F32)).astype(BF16)
+    swap(1, layers - 1, upstream)
     for l in range(layers - 1, 0, -1):
-        pair_send(2 + l, dot_nt(gp, weight(l, True)).astype(BF16))
-        small_send(l - 1, jnp.sum(gp.astype(F32) * projs[l].astype(F32), axis=1, keepdims=True))
-        wgrad(l, gp)
-        rs_start(l)
-        if l < layers - 1:
-            rs_tick()
-        grad_normed = pair_recv(2 + l)
+        turns = RING_STEPS[layers - 1 - l]
+        swap(3, l, gp)
+        grad_normed = backward_dot(gp, l, 0)
         inverse = rcols[l, :, 0:1]
-        inner = small_recv(l - 1) * (inverse * inverse) / width
-        gcur[...] = (
-            gcur[...].astype(F32) + inverse * gain(l) * grad_normed - xs[l].astype(F32) * inner
+        inner = jnp.sum(gp.astype(F32) * projs[l].astype(F32), axis=1, keepdims=True)
+        inner = inner * (inverse * inverse) / width
+        upstream = (
+            upstream.astype(F32) + inverse * gain(l) * grad_normed - xs[l].astype(F32) * inner
         ).astype(BF16)
-        ar_send(4 + l, dot_nn(gcur[...], weight(l - 1, False)).astype(BF16))
-        rs_tick()
-        rs_tick()
+        ar_send(4 + l, forward_dot(upstream, l - 1, 1).astype(BF16))
+        swap(1, l - 1, upstream)
+        if l == layers - 1:
+            wgrad_output(l)
+        wgrad_value(l)
+        rs_ticks(turns[0])
+        wgrad_output(l - 1)
+        rs_ticks(turns[1])
         gp = ar_recv(4 + l).astype(BF16)
-    wgrad(0, gp)
-    rs_start(0)
+    swap(3, 0, gp)
+    rs_ticks(1)
+    wgrad_value(0)
     while any(i <= steps for i in position.values()):
         rs_tick()
 
@@ -468,42 +509,45 @@
         in_specs=[anywhere] * 4 + [vmem] * 7,
         out_specs=vmem,
         scratch_shapes=[
-            pltpu.VMEM((2 * rows + 16, width), BF16),
+            pltpu.VMEM((rows + 16, width), BF16),
             pltpu.VMEM((ns, 1, width), F32),
             pltpu.VMEM((ns, n, sub, 2 * half), BF16),
+            pltpu.VMEM((ns, n, sub, 2 * half), BF16),
             pltpu.VMEM((ns, q), F32),
-            pltpu.VMEM((n, 8, rows), F32),
-            pltpu.VMEM((ns, rows, q), BF16),
-            pltpu.VMEM((rows, q), BF16),
-            pltpu.VMEM((ns, rows, half), BF16),
-            pltpu.VMEM((ns, rows, 128), F32),
-            pltpu.VMEM((rows, q), BF16),
+            pltpu.VMEM((n, 8, 128), F32),
+            pltpu.VMEM((ns, rows // 2, q), BF16),
+            pltpu.VMEM((rows // 2, q), BF16),
+            pltpu.VMEM((ns, rows // 2, 2 * half), BF16),
+            pltpu.VMEM((ns, rows // 2, 128), F32),
             pltpu.VMEM((ns, n, sub, 2 * half), BF16),
             pltpu.VMEM((ns, steps, sub, 2 * half), BF16),
             pltpu.VMEM((ns, steps, sub, 2 * half), BF16),
             pltpu.VMEM((ns, sub, 2 * half), BF16),
             pltpu.VMEM((ns, sub, 2 * half), BF16),
-            pltpu.VMEM((8, rows, half), BF16),
-            pltpu.VMEM((8, ns - 1, rows, half), BF16),
-            pltpu.VMEM((ns, 8, rows), F32),
-            pltpu.VMEM((ns, ns - 1, 8, rows), F32),
-            pltpu.VMEM((6, rows, q), BF16),
-            pltpu.VMEM((6, rows, q), BF16),
-            pltpu.VMEM((4, 8, rows), F32),
-            pltpu.VMEM((4, 8, rows), F32),
-            pltpu.VMEM((3, rows, 128), F32),
+            pltpu.VMEM((8, rows // 2, 2 * half), BF16),
+            pltpu.VMEM((8, ns - 1, rows // 2, 2 * half), BF16),
+            pltpu.VMEM((ns, 8, 128), F32),
+            pltpu.VMEM((ns, ns - 1, 8, 128), F32),
+            pltpu.VMEM((ns, rows, q), BF16),
+            pltpu.VMEM((ns, rows, q), BF16),
+            pltpu.VMEM((ns, rows, half), BF16),
+            pltpu.VMEM((ns, rows, half), BF16),
+            pltpu.VMEM((ns, rows // 2, half), BF16),
+            pltpu.VMEM((ns, rows // 2, half), BF16),
+            pltpu.VMEM((3, rows // 2, 128), F32),
+            pltpu.VMEM((ns, math.lcm(sub, 128), math.lcm(sub, 128)), BF16),
             dma((4,)), dma((2, ns - 1)), dma((2, ns)), dma((ns - 1,)), dma((ns,)),
             dma((ns, 2, 2, steps)), dma((ns, 2, 2, steps)), dma((2, steps)), dma((2, steps)),
             dma((8, ns - 1)), dma((8, ns - 1)), dma((ns, ns - 1)), dma((ns, ns - 1)),
-            dma((6,)), dma((6,)), dma((4,)), dma((4,)),
+            dma((ns, n)), dma((ns, n)), dma((4, ns)), dma((4, ns)),
             dma((ns, 2, 2, steps)), dma((ns, 2, 2, steps)), dma((ns,)), dma((ns,)),
         ],
         compiler_params=pltpu.CompilerParams(
             collective_id=0, has_side_effects=True, vmem_limit_bytes=60 * 1024 * 1024
         ),
     )(
-        hidden.reshape(rows, width),
-        unembed.reshape(rows, width),
+        hidden.reshape(2, rows // 2, width),
+        unembed.reshape(2, rows // 2, width),
         value_proj.reshape(ns, sub, half),
         output_proj[0].T.reshape(ns, sub, half),
         norm_gains,

time: 191 us -> 188 us (0.984)
  Pallas kernels: 187 us -> 184 us
    pallas_call x1, Pallas kernels: 187 us -> 184 us  [local(): pl.pallas_call(functools.partial(kernel, dims), out_shape=jax.ShapeDtypeS...]
where the time goes in v3:
time: 188 us
  Pallas kernels  184 us (98%)
  local copies, waits for them, and re-layouts  1.95 us (1%)
    pallas_call x1, Pallas kernels, local(): pl.pallas_call(functools.partial(kernel, dims), out_shape=jax.ShapeDtypeS...  184 us

profile of v3, /device:TPU:40, one launch (start us, length us, event | category | flops | bytes accessed | tf_op | source)
XLA Modules:
  0.0 187.7 jit_solution(8935104115755976321)
XLA Ops:
  1.3 184.5 %shard_map.122 = f32[4,80,512]{2,1,0:T(8,128)} custom-call(bf16[2,64,5120]{2,1,0:T(8,128)(2,1)} %bitcast.23, bf16[2,64,5120]{2,1,0:T(8,128)(2,1)} %bitcast.24, bf16[4,80,256]{2,1,0:T(8,128)(2,1)} %bitcast.25, bf16[4,80,256]{2,1,0:T(8,128)(2,1)} %bitcast.26, f32[1,5120]{1,0:T(1,128)} %gown.1, s32[1,1]{1,0:T(1,128)} %bitcast.21.surv, s32[1,16]{1,0:T(1,128)} %bitcast.29, ...), custom_call_target="tpu_custom_call" | custom-call | tf_op jit(solution)/shard_map/pallas_call | solution.py:506
  185.8 1.9 %slice_bitcast_fusion = (f32[1,256,320]{1,2,0:T(8,128)}, f32[1,320,256]{2,1,0:T(8,128)}) fusion(f32[320,512]{1,0:T(8,128)} %bitcast.22), kind=kLoop, calls=%fused_computation | loop fusion | bytes 1310720 | tf_op jit(solution)/shard_map/broadcast_in_dim | solution.py:562

commit v4 on v3

--- a/solution.py
+++ b/solution.py
@@ -447,6 +447,9 @@
         turns = RING_STEPS[layers - 1 - l]
         swap(3, l, gp)
         grad_normed = backward_dot(gp, l, 0)
+        if l == layers - 1:
+            wgrad_output(l)
+            wgrad_value(l)
         inverse = rcols[l, :, 0:1]
         inner = jnp.sum(gp.astype(F32) * projs[l].astype(F32), axis=1, keepdims=True)
         inner = inner * (inverse * inverse) / width
@@ -455,9 +458,8 @@
         ).astype(BF16)
         ar_send(4 + l, forward_dot(upstream, l - 1, 1).astype(BF16))
         swap(1, l - 1, upstream)
-        if l == layers - 1:
-            wgrad_output(l)
-        wgrad_value(l)
+        if l < layers - 1:
+            wgrad_value(l)
         rs_ticks(turns[0])
         wgrad_output(l - 1)
         rs_ticks(turns[1])

time: 188 us -> 190 us (1.011)
  Pallas kernels: 184 us -> 186 us
where the time goes in v4:
time: 190 us; the launch traced here: 189 us
  Pallas kernels  186 us (98%)
  local copies, waits for them, and re-layouts  1.95 us (1%)
    pallas_call x1, Pallas kernels, local(): pl.pallas_call(functools.partial(kernel, dims), out_shape=jax.ShapeDtypeS...  186 us

profile of v4, /device:TPU:40, one launch (start us, length us, event | category | flops | bytes accessed | tf_op | source)
XLA Modules:
  0.0 189.4 jit_solution(1904310897181739470)
XLA Ops:
  1.3 186.2 %shard_map.122 = f32[4,80,512]{2,1,0:T(8,128)} custom-call(bf16[2,64,5120]{2,1,0:T(8,128)(2,1)} %bitcast.23, bf16[2,64,5120]{2,1,0:T(8,128)(2,1)} %bitcast.24, bf16[4,80,256]{2,1,0:T(8,128)(2,1)} %bitcast.25, bf16[4,80,256]{2,1,0:T(8,128)(2,1)} %bitcast.26, f32[1,5120]{1,0:T(1,128)} %gown.1, s32[1,1]{1,0:T(1,128)} %bitcast.21.surv, s32[1,16]{1,0:T(1,128)} %bitcast.29, ...), custom_call_target="tpu_custom_call" | custom-call | tf_op jit(solution)/shard_map/pallas_call | solution.py:508
  187.5 1.9 %slice_bitcast_fusion = (f32[1,256,320]{1,2,0:T(8,128)}, f32[1,320,256]{2,1,0:T(8,128)}) fusion(f32[320,512]{1,0:T(8,128)} %bitcast.22), kind=kLoop, calls=%fused_computation | loop fusion | bytes 1310720 | tf_op jit(solution)/shard_map/broadcast_in_dim | solution.py:564
